TPU v7x, 32 devices: a whole 2x2x4 slice. The times are simulated.
32 devices in a mesh: row: 4 (over z), col: 4 (over x, core), ch: 2 (over y).
Axes of the slice: x: 2, y: 2, z: 4, core: 2. Of those that a mesh axis runs over, the one named last changes fastest.
Arguments:
- image_tokens: bfloat16 [64, 1024, 128], P(('row', 'ch'), 'col'), may hold values from -61 to 61
- labels: int32 [64, 1024], P(('row', 'ch'), 'col'), may hold values from 0 to 2
- rel_index: int32 [64, 64], replicated, may hold values from 0 to 224
- norm_gain: float32 [2, 2, 128], replicated, may hold values from 0.25 to 1.75
- norm_shift: float32 [2, 2, 128], replicated, may hold values from -1.5 to 1.5
- qkv_weight: bfloat16 [2, 3, 128, 128], P(None, None, None, 'ch'), may hold values from -5 to 5
- qkv_bias: float32 [2, 3, 128], P(None, None, 'ch'), may hold values from -1.5 to 1.5
- bias_table: float32 [2, 225, 4], P(None, None, 'ch'), may hold values from -4 to 4
- proj_weight: bfloat16 [2, 128, 128], P(None, 'ch'), may hold values from -0.5 to 0.5
- proj_bias: float32 [2, 128], replicated, may hold values from -1.5 to 1.5
- fc1_weight: bfloat16 [2, 128, 512], P(None, None, 'ch'), may hold values from -0.5 to 0.5
- fc1_bias: float32 [2, 512], P(None, 'ch'), may hold values from -2.5 to 2.5
- fc2_weight: bfloat16 [2, 512, 128], P(None, 'ch'), may hold values from -0.25 to 0.25
- fc2_bias: float32 [2, 128], replicated, may hold values from -1.5 to 1.5
Outputs:
- encoded: bfloat16 [64, 1024, 128], P(('row', 'ch'), 'col')
All inputs are finite; a program needn't handle non-finite values.
Results may differ from a plain program's by a relative error of at most 0.014.
Values may be sent and summed in bfloat16 or wider, within the bound.
A program may use at most 128 MiB of HBM per device.

v0:
```python
import functools

import jax
import jax.numpy as jnp
from jax import lax
from jax.experimental import pallas as pl
from jax.experimental.pallas import tpu as pltpu
from jax.sharding import PartitionSpec as P

WIN = 8
SHIFT = 4
BLOCKS = 2
EPS = 1e-05
FAR = -1e30
LOG2E = 1.4426950408889634
GROUP = 22
bf16 = jnp.bfloat16
f32 = jnp.float32


def dot(a, b):
    return jnp.dot(a, b, preferred_element_type=f32)


def dot_t(a, b):
    return lax.dot_general(a, b, (((1,), (1,)), ((), ())), preferred_element_type=f32)


def layer_norm(x, gain, offset):
    center = x - jnp.mean(x, axis=-1, keepdims=True)
    spread = jnp.mean(center * center, axis=-1, keepdims=True)
    return (center * lax.rsqrt(spread + EPS) * gain + offset).astype(bf16)


def rows_of(x):
    return x.reshape(x.shape[0] * x.shape[1], x.shape[2])


def attend(group, hmask, heads, depth):
    keys, width = group[0][1].shape
    per = 128 // keys
    scores, values = [], []
    for q, k, v, far, _ in group:
        kb = jnp.concatenate([k] * heads, axis=0) * hmask
        if far is not None:
            q = jnp.concatenate([q, far[0]], axis=1)
            kb = jnp.concatenate([kb, jnp.concatenate([far[1]] * heads, axis=0)], axis=1)
        scores.append(dot_t(q, kb))
        values.append(jnp.concatenate([jnp.concatenate([v] * heads, axis=0) * hmask, hmask], axis=1))
    lane = lax.broadcasted_iota(jnp.int32, (scores[0].shape[0], 128), 1)
    weights = []
    for s, (_, _, _, _, bias) in zip(scores, group):
        s = s * (depth ** (-0.5) * LOG2E) + bias
        parts = []
        for c in range(0, s.shape[1], 128):
            t = s[:, c : c + 128]
            top = None
            for j in range(per):
                inside = (lane >= j * keys) & (lane < (j + 1) * keys)
                peak = jnp.max(jnp.where(inside, t, -jnp.inf), axis=-1, keepdims=True)
                top = peak if top is None else jnp.where(lane >= j * keys, peak, top)
            parts.append(jnp.exp2(t - top))
        weights.append(jnp.concatenate(parts, axis=1).astype(bf16))
    outs = [dot(p, v) for p, v in zip(weights, values)]
    return [(o[:, :width] / o[:, width:]).astype(bf16) for o in outs]


def finish(x, attended, w, b):
    mixed = dot(attended, w["proj"][b])
    middle = (x + mixed + w["proj_b"][b]).astype(bf16).astype(f32)
    normed = layer_norm(middle, w["gain"][b][1:2], w["shift"][b][1:2])
    inner = dot(normed, w["fc1"][b]) + w["fc1_b"][b]
    hidden = (0.5 * inner * (1.0 + lax.erf(inner * (0.5 ** 0.5)))).astype(bf16)
    outer = dot(hidden, w["fc2"][b])
    return (middle + outer + w["fc2_b"][b]).astype(bf16)


def head_mask(heads, keys, width):
    depth = width // heads
    row = lax.broadcasted_iota(jnp.int32, (heads * keys, width), 0) // keys
    col = lax.broadcasted_iota(jnp.int32, (heads * keys, width), 1) // depth
    return (row == col).astype(f32).astype(bf16)


def qkv_of(x, w, b):
    normed = layer_norm(x, w["gain"][b][0:1], w["shift"][b][0:1])
    return dot_t(normed, rows_of(w["qkv"][b])) + w["qkv_b"][b]


def first_chunk(x, w, heads, hmask):
    rows, wide, width = x.shape
    depth = width // heads
    toks = jnp.concatenate(
        [rows_of(x[:, c : c + WIN]) for c in range(0, wide, WIN)], axis=0
    )
    triple = qkv_of(toks, w, 0)
    outs = []
    n = WIN * WIN
    windows = []
    for g in range(wide // WIN):
        t = triple[g * n : (g + 1) * n].astype(bf16)
        windows.append((t[:, :width], t[:, width : 2 * width], t[:, 2 * width :], None, w["bias"][0]))
    for g in range(0, len(windows), GROUP):
        outs += attend(windows[g : g + GROUP], hmask, heads, depth)
    return finish(toks, jnp.concatenate(outs, axis=0), w, 0)


def second_chunk(x, reg, w, heads, hmask):
    kinds = lax.broadcasted_iota(jnp.int32, (WIN * WIN, 128), 1).astype(f32)
    rows, wide, width = x.shape
    depth = width // heads
    half = WIN // 2
    outs, toks, windows = [], [], []
    n = WIN * WIN
    for r in range(0, rows, WIN):
        xs = [rows_of(x[r : r + WIN, c : c + WIN]) for c in range(0, wide, WIN)]
        same = [(rows_of(reg[r : r + WIN, c : c + WIN]) == kinds).astype(f32) for c in range(0, wide, WIN)]
        triple = qkv_of(jnp.concatenate(xs, axis=0), w, 1)
        own = slice(half * WIN, n) if r == 0 else slice(0, half * WIN)
        bias = w["bias"][1][own, :]
        for g in range(wide // WIN):
            t = triple[g * n : (g + 1) * n].astype(bf16)
            far = (same[g][own] * FAR).astype(bf16), (1.0 - same[g]).astype(bf16)
            windows.append((t[own, :width], t[:, width : 2 * width], t[:, 2 * width :], far, bias))
            toks.append(xs[g][own])
    for g in range(0, len(windows), GROUP):
        outs += attend(windows[g : g + GROUP], hmask, heads, depth)
    return finish(jnp.concatenate(toks, axis=0), jnp.concatenate(outs, axis=0), w, 1)


def fused(
    heads, chunk0, chunk1,
    x_ref, lab_ref, rel_ref, gain, shift, qkv_w, qkv_b, table, proj_w, proj_b, fc1_w, fc1_b, fc2_w, fc2_b,
    o_ref,
    ext, regb, res, x1, top, bot, side, corner, lab, tab_own, tab_all,
    qb_all, f1b_all, qkv, qb, bias, proj, fc1, f1b, fc2,
    wsend, wrecv, rsend, rrecv, lsend, lrecv, hsend, hrecv, esend, erecv, own_sem,
):
    rows, cols, width = x_ref.shape
    n = lax.axis_size("ch")
    nrow, ncol = lax.axis_size("row"), lax.axis_size("col")
    row, col, ch = lax.axis_index("row"), lax.axis_index("col"), lax.axis_index("ch")
    ring = row * n + ch
    total = nrow * n

    def at(dr, dc):
        p = lax.rem(ring + dr + total, total)
        return (p // n, lax.rem(col + dc + ncol, ncol), lax.rem(p, n))

    around = [(-1, -1), (-1, 0), (-1, 1), (0, -1), (0, 1), (1, -1), (1, 0), (1, 1)]
    peers = [(row, col, lax.rem(ch + d, n)) for d in range(1, n)]
    mate = (row, col + 1 - 2 * lax.rem(col, 2), ch)
    core = lax.rem(col, 2)
    mesh_id = pl.DeviceIdType.MESH

    barrier = pltpu.get_barrier_semaphore()
    targets = [at(*d) for d in around] + peers + [mate]
    for t in targets:
        pl.semaphore_signal(barrier, inc=1, device_id=t, device_id_type=mesh_id)

    def remote(src, dst, ssem, rsem, to):
        return pltpu.make_async_remote_copy(
            src_ref=src, dst_ref=dst, send_sem=ssem, recv_sem=rsem, device_id=to, device_id_type=mesh_id
        )

    tab_own[...] = jnp.zeros_like(tab_own)
    tab_own[:, : table.shape[1], : table.shape[2]] = table[...]
    pl.semaphore_wait(barrier, len(targets))

    part = width // n
    kh, ph, fh, gh = qkv_w.shape[2] // 2, proj_w.shape[1] // 2, width // 2, fc2_w.shape[1] // 2
    pw, fw, gw = proj_w.shape[1], fc1_w.shape[2], fc2_w.shape[1]

    def pieces(b, owner):
        k0, p0, f0, g0 = (pl.multiple_of(core * v, 16) for v in (kh, ph, fh, gh))
        return [
            (qkv_w.at[b, :, pl.ds(k0, kh), :], qkv.at[b, :, pl.ds(pl.multiple_of(owner * part + k0, 16), kh), :]),
            (proj_w.at[b, pl.ds(p0, ph), :], proj.at[b, pl.ds(pl.multiple_of(owner * pw + p0, 16), ph), :]),
            (
                fc1_w.at[b, pl.ds(f0, fh), :],
                fc1.at[b, pl.ds(f0, fh), pl.ds(pl.multiple_of(owner * fw, 128), fw)],
            ),
            (fc2_w.at[b, pl.ds(g0, gh), :], fc2.at[b, pl.ds(pl.multiple_of(owner * gw + g0, 16), gh), :]),
        ]

    direct, relays, smalls = {}, {}, []
    for d in range(1, n):
        to, owner = peers[d - 1], lax.rem(ch - d + n, n)
        for b in range(BLOCKS):
            for i, (src, dst) in enumerate(pieces(b, ch)):
                direct[d, b, i] = remote(src, dst, wsend.at[d - 1, b, i], wrecv.at[d - 1, b, i], to)
            for i, (_, dst) in enumerate(pieces(b, owner)):
                relays[d, b, i] = remote(dst, dst, rsend.at[d - 1, b, i], rrecv.at[d - 1, b, i], mate)
        for i, (src, dst) in enumerate(
            [(tab_own, tab_all.at[ch]), (qkv_b, qb_all.at[ch]), (fc1_b, f1b_all.at[ch])]
        ):
            smalls.append(remote(src, dst, wsend.at[d - 1, BLOCKS, i], wrecv.at[d - 1, BLOCKS, i], to))
    for c in smalls:
        c.start()
    for d in range(1, n):
        for i in range(4):
            direct[d, 0, i].start()
    labels = []
    for i, d in enumerate(around):
        labels.append(remote(lab_ref, lab.at[i], lsend.at[i], lrecv.at[i], at(-d[0], -d[1])))
        labels[-1].start()
    for d in range(1, n):
        for i in range(4):
            direct[d, 1, i].start()
    locals_ = [
        (qkv_w, qkv.at[:, :, pl.ds(pl.multiple_of(ch * part, 16), part), :]),
        (proj_w, proj.at[:, pl.ds(pl.multiple_of(ch * pw, 16), pw), :]),
        (fc1_w, fc1.at[:, :, pl.ds(pl.multiple_of(ch * fw, 128), fw)]),
        (fc2_w, fc2.at[:, pl.ds(pl.multiple_of(ch * gw, 16), gw), :]),
        (tab_own, tab_all.at[ch]), (qkv_b, qb_all.at[ch]), (fc1_b, f1b_all.at[ch]),
    ]
    locals_ = [pltpu.make_async_copy(s, d, own_sem.at[i]) for i, (s, d) in enumerate(locals_)]
    for c in locals_:
        c.start()
    for c in locals_:
        c.wait()
    for c in smalls:
        c.wait()

    keys = WIN * WIN
    for j in range(n):
        for b in range(BLOCKS):
            for m in range(3):
                qb[b, :, m * width + j * part : m * width + (j + 1) * part] = qb_all[j, m, b : b + 1, :]
            f1b[b, :, j * fw : (j + 1) * fw] = f1b_all[j, b : b + 1, :]
    local_heads = table.shape[1]
    per = 128 // keys
    idx = jnp.concatenate([rel_ref[...]] * per, axis=1)
    lane = lax.broadcasted_iota(jnp.int32, idx.shape, 1)
    for b in range(BLOCKS):
        for t in range(heads // per):
            out = None
            for j in range(per):
                h = t * per + j
                entry = tab_all[h // local_heads, b, h % local_heads : h % local_heads + 1, :]
                got = None
                for c in range(0, entry.shape[1], 128):
                    piece = jnp.broadcast_to(entry[:, c : c + 128], idx.shape)
                    here = jnp.take_along_axis(piece, idx & 127, axis=1, mode="promise_in_bounds")
                    got = here if got is None else jnp.where(idx >= c, here, got)
                out = got if out is None else jnp.where(lane >= j * keys, got, out)
            bias[b, :, t * 128 : (t + 1) * 128] = out * LOG2E

    def bring(b):
        for d in range(1, n):
            for i in range(4):
                direct[d, b, i].wait_recv()
                relays[d, b, i].start()

    def settle(b):
        for d in range(1, n):
            for i in range(4):
                relays[d, b, i].wait_recv()

    bring(0)
    settle(0)
    w = {
        "gain": gain, "shift": shift, "qkv": qkv, "qkv_b": qb, "bias": bias, "proj": proj,
        "proj_b": [proj_b[b : b + 1] for b in range(BLOCKS)], "fc1": fc1, "fc1_b": f1b, "fc2": fc2,
        "fc2_b": [fc2_b[b : b + 1] for b in range(BLOCKS)],
    }
    hmask = head_mask(heads, keys, width)

    def halo(k):
        span = pl.ds(pl.multiple_of(k * chunk0, chunk0), chunk0)
        return [
            remote(x1.at[rows - SHIFT :, span, :], top.at[:, span, :], hsend.at[0, k], hrecv.at[0, k], at(1, 0)),
            remote(x1.at[:SHIFT, span, :], bot.at[:, span, :], hsend.at[1, k], hrecv.at[1, k], at(-1, 0)),
        ]

    def regular(step, _):
        k = lax.rem(step + 1, cols // chunk0)
        span = pl.ds(pl.multiple_of(k * chunk0, chunk0), chunk0)
        y = first_chunk(x_ref[:, span, :].astype(f32), w, heads, hmask).astype(f32)
        m = WIN * WIN
        y = jnp.concatenate(
            [y[g * m : (g + 1) * m].reshape(WIN, WIN, width) for g in range(chunk0 // WIN)], axis=1
        )
        x1[:, span, :] = y.astype(bf16)
        for c in halo(k):
            c.start()
        return 0

    lax.fori_loop(0, cols // chunk0, regular, 0)
    edge = side.shape[2]
    edges = []
    for s, dc in ((0, 1), (1, -1)):
        span = slice(cols - edge, cols) if dc == 1 else slice(0, edge)
        edges.append(remote(x1.at[:, span, :], side.at[s], esend.at[s, 0], erecv.at[s, 0], at(0, dc)))
        edges.append(
            remote(x1.at[rows - SHIFT :, span, :], corner.at[s, 0], esend.at[s, 1], erecv.at[s, 1], at(1, dc))
        )
        edges.append(remote(x1.at[:SHIFT, span, :], corner.at[s, 1], esend.at[s, 2], erecv.at[s, 2], at(-1, dc)))
    for c in edges:
        c.start()
    bring(1)
    for c in labels:
        c.wait()
    def column(up, mid, down):
        return jnp.concatenate([up[rows - SHIFT :], mid, down[:SHIFT]], axis=0)
    west = column(lab[0], lab[3], lab[5]).astype(f32)
    mid = column(lab[1], lab_ref[...], lab[6]).astype(f32)
    east = column(lab[2], lab[4], lab[7]).astype(f32)
    tall = rows + 2 * SHIFT
    moved = pltpu.roll(jnp.concatenate([mid, jnp.zeros((tall, 128), f32)], axis=1), SHIFT, 1)
    span = cols + 128
    j = lax.broadcasted_iota(jnp.int32, (tall, span), 1)
    i = lax.broadcasted_iota(jnp.int32, (tall, span), 0)
    blank = jnp.zeros((tall, span - 128), f32)
    left = jnp.concatenate([pltpu.roll(west[:, cols - 128 :], SHIFT, 1), blank], axis=1)
    right = jnp.concatenate([blank, pltpu.roll(east[:, :128], SHIFT, 1)], axis=1)
    kind = jnp.where(j < SHIFT, left, jnp.where(j < cols + SHIFT, moved, right))
    def flag(here, when):
        return jnp.where(here, when.astype(f32), 0.0)
    low = flag((i >= SHIFT) & (i < 2 * SHIFT), ring == 0) + flag(i >= rows + SHIFT, ring == total - 1)
    front = flag((j >= SHIFT) & (j < 2 * SHIFT), col == 0) + flag(j >= cols + SHIFT, col == ncol - 1)
    kind = kind * 4.0 + low * 2.0 + front
    turned = kind.T[: cols + 2 * SHIFT].astype(bf16)
    pick = lax.broadcasted_iota(jnp.int32, (tall, 128), 0)
    for r in range(tall):
        regb[r] = dot(turned, (pick == r).astype(f32).astype(bf16))
    settle(1)
    ext[SHIFT : SHIFT + rows, SHIFT : SHIFT + cols, :] = x1[...].astype(f32)
    def land(k):
        span = slice(k * chunk0, (k + 1) * chunk0)
        put = slice(SHIFT + k * chunk0, SHIFT + (k + 1) * chunk0)
        for c in halo(k):
            c.wait()
        ext[:SHIFT, put, :] = top[:, span, :].astype(f32)
        ext[SHIFT + rows :, put, :] = bot[:, span, :].astype(f32)

    half = WIN // 2

    def shifted(k, _):
        span = pl.ds(pl.multiple_of(k * chunk1, WIN), chunk1)
        y = second_chunk(ext[:, span, :], regb[:, span, :], w, heads, hmask).astype(f32)
        m = half * WIN
        g = chunk1 // WIN
        for r in range(2):
            for q in range(g):
                e = (r * g + q) * m
                place = pl.ds(pl.multiple_of(k * chunk1 + q * WIN, WIN), WIN)
                res[r * half : (r + 1) * half, place, :] = y[e : e + m].reshape(half, WIN, width)
        return 0

    steps = (cols + 2 * SHIFT) // chunk1
    first, last = (chunk1 - SHIFT) // chunk0, ((steps - 1) * chunk1 - SHIFT - 1) // chunk0
    ready = range(first, last + 1) if steps > 2 else ()
    for k in ready:
        land(k)
    if steps > 2:
        lax.fori_loop(1, steps - 1, shifted, 0)
    for k in range(cols // chunk0):
        if k not in ready:
            land(k)
    for c in edges:
        c.wait()
    for s in range(2):
        take = slice(edge - SHIFT, edge) if s == 0 else slice(0, SHIFT)
        put = slice(0, SHIFT) if s == 0 else slice(SHIFT + cols, 2 * SHIFT + cols)
        ext[SHIFT : SHIFT + rows, put, :] = side[s].astype(f32)[:, take, :]
        ext[:SHIFT, put, :] = corner[s, 0].astype(f32)[:, take, :]
        ext[SHIFT + rows :, put, :] = corner[s, 1].astype(f32)[:, take, :]
    if steps > 1:
        lax.fori_loop(0, 2, lambda i, c: shifted(i * (steps - 1), c), 0)
    else:
        shifted(0, 0)
    o_ref[...] = res[:, SHIFT : SHIFT + cols, :].astype(bf16)
    for c in list(direct.values()) + list(relays.values()):
        c.wait_send()


def chunk_of(windows, most):
    return max(d for d in range(1, most + 1) if windows % d == 0) * WIN


def on_device(*args):
    x, labels, rel_index = args[:3]
    qkv_weight, qkv_bias, bias_table, proj_weight = args[5:9]
    fc1_weight, fc1_bias, fc2_weight = args[10:13]
    rows, cols, width = x.shape
    n = lax.axis_size("ch")
    heads = bias_table.shape[2] * n
    args = list(args)
    args[5] = qkv_weight.swapaxes(2, 3)
    args[6] = qkv_bias.swapaxes(0, 1)
    args[7] = bias_table.swapaxes(1, 2)
    hidden = fc1_weight.shape[2] * n
    chunk0, chunk1 = chunk_of(cols // WIN, 4), chunk_of(cols // WIN + 1, 11)
    tall, wide = rows + 2 * SHIFT, cols + 2 * SHIFT
    edge, keys = 16, WIN * WIN
    dma = pltpu.SemaphoreType.DMA
    vm = pltpu.VMEM
    entries = bias_table.shape[1] + -bias_table.shape[1] % 128
    scratch = [
        vm((tall, wide, width), f32), vm((tall, wide, 128), f32), vm((rows, wide, width), f32),
        vm((rows, cols, width), bf16), vm((SHIFT, cols, width), bf16), vm((SHIFT, cols, width), bf16),
        vm((2, rows, edge, width), bf16), vm((2, 2, SHIFT, edge, width), bf16), vm((8, rows, cols), jnp.int32),
        vm((BLOCKS, 8, entries), f32), vm((n, BLOCKS, 8, entries), f32),
        vm((n,) + args[6].shape, f32), vm((n,) + fc1_bias.shape, f32),
        vm((BLOCKS, 3, width, width), bf16), vm((BLOCKS, 1, 3 * width), f32),
        vm((BLOCKS, keys, heads * keys), f32), vm((BLOCKS, width, width), bf16),
        vm((BLOCKS, width, hidden), bf16), vm((BLOCKS, 1, hidden), f32), vm((BLOCKS, hidden, width), bf16),
        dma((n - 1, BLOCKS + 1, 4)), dma((n - 1, BLOCKS + 1, 4)),
        dma((n - 1, BLOCKS, 4)), dma((n - 1, BLOCKS, 4)),
        dma((8,)), dma((8,)), dma((2, cols // chunk0)), dma((2, cols // chunk0)), dma((2, 3)), dma((2, 3)),
        dma((7,)),
    ]
    vmem = pl.BlockSpec(memory_space=vm)
    return pl.pallas_call(
        functools.partial(fused, heads, chunk0, chunk1),
        out_shape=jax.ShapeDtypeStruct(x.shape, bf16),
        in_specs=[vmem] * len(args),
        out_specs=vmem,
        scratch_shapes=scratch,
        compiler_params=pltpu.CompilerParams(
            collective_id=0, has_side_effects=True, vmem_limit_bytes=60 * 1024 * 1024
        ),
        name="fused",
    )(*args)


def solution(mesh):
    in_specs = (
        P(("row", "ch"), "col", None), P(("row", "ch"), "col"), P(), P(), P(),
        P(None, None, None, "ch"), P(None, None, "ch"), P(None, None, "ch"), P(None, "ch", None), P(),
        P(None, None, "ch"), P(None, "ch"), P(None, "ch", None), P(),
    )
    out_specs = P(("row", "ch"), "col", None)
    return jax.shard_map(on_device, mesh=mesh, in_specs=in_specs, out_specs=out_specs, check_vma=False)
```

profile of v0, /device:TPU:0, one launch (start us, length us, event | category | flops | bytes accessed | tf_op | source)
XLA Modules:
  0.0 39.5 jit_solution(12628997326332243945)
XLA Ops:
  0.0 37.6 %fused.1 = bf16[8,256,128]{2,1,0:T(8,128)(2,1)} custom-call(bf16[8,256,128]{2,1,0:T(8,128)(2,1)} %x_ref.1, s32[8,256]{1,0:T(8,128)} %lab_ref.1, s32[64,64]{1,0:T(8,128)} %rel_ref.1, f32[2,2,128]{2,1,0:T(2,128)} %gain.1, f32[2,2,128]{2,1,0:T(2,128)} %shift.1, bf16[2,3,64,128]{3,2,1,0:T(8,128)(2,1)} %bitcast.3, f32[3,2,64]{2,1,0:T(2,128)} %bitcast.5, ...), custom_call_target="tpu_custom_call" | custom-call | tf_op jit(solution)/shard_map/fused/pallas_call | solution.py:415
  37.6 1.9 %copy.16 = bf16[8,256,128]{2,1,0:T(8,128)(2,1)} copy(bf16[8,256,128]{2,1,0:T(8,128)(2,1)} %fused.1) | data formatting | bytes 1048576
where the time goes:
time: 39.7 us; the launch traced here: 39.5 us
  Pallas kernels  37.6 us (95%)
  local copies, waits for them, and re-layouts  1.87 us (5%)
    pallas_call x1, Pallas kernels, on_device(): pl.pallas_call(functools.partial(fused, heads, chunk0, chunk1), out_shape...  37.6 us
    unnamed x1, local copies, waits for them, and re-layouts  1.87 us

commit v1 on v0

v1 whole, which is shorter than its diff:
```python
import functools

import jax
import jax.numpy as jnp
from jax import lax
from jax.experimental import pallas as pl
from jax.experimental.pallas import tpu as pltpu
from jax.sharding import PartitionSpec as P

WIN = 8
SHIFT = 4
BLOCKS = 2
EPS = 1e-05
FAR = -1e30
LOG2E = 1.4426950408889634
MOST = 8
bf16 = jnp.bfloat16
f32 = jnp.float32
i32 = jnp.int32
KEYS = WIN * WIN
PART = SHIFT * SHIFT


def dot(a, b):
    return jnp.dot(a, b, preferred_element_type=f32)


def dot_t(a, b):
    return lax.dot_general(a, b, (((1,), (1,)), ((), ())), preferred_element_type=f32)


def layer_norm(x, gain, offset):
    center = x - jnp.mean(x, axis=-1, keepdims=True)
    spread = jnp.mean(center * center, axis=-1, keepdims=True)
    return (center * lax.rsqrt(spread + EPS) * gain + offset).astype(bf16)


def rows_of(x):
    return x.reshape(x.shape[0] * x.shape[1], x.shape[2])


def swap_halves(e, o):
    low = lax.broadcasted_iota(i32, e.shape, 1) < SHIFT
    return jnp.where(low, e, pltpu.roll(o, SHIFT, 1)), jnp.where(low, pltpu.roll(e, SHIFT, 1), o)


def quads(x):
    rows, wide, width = x.shape
    g = wide // WIN
    pairs = []
    for r in range(0, rows, 2):
        pairs.append(swap_halves(x[r].reshape(g, WIN, width), x[r + 1].reshape(g, WIN, width)))
    parts = []
    for w in range(g):
        for h in range(0, rows // 2, 2):
            parts += [pairs[h + i][s][w] for s in (0, 1) for i in (0, 1)]
    return jnp.concatenate(parts, axis=0)


def place_of(t):
    q, i = t >> 4, t & 15
    return SHIFT * (q >> 1) + (i >> 2), SHIFT * (q & 1) + (i & 3)


def head_mask(heads, keys, width):
    depth = width // heads
    row = lax.broadcasted_iota(i32, (heads * keys, width), 0) // keys
    col = lax.broadcasted_iota(i32, (heads * keys, width), 1) // depth
    return (row == col).astype(f32).astype(bf16)


def scores_of(triple, hmask, heads):
    width = triple.shape[1] // 3
    out = []
    for w in range(0, triple.shape[0], KEYS):
        q, k = triple[w : w + KEYS, :width], triple[w : w + KEYS, width : 2 * width]
        out.append(dot_t(q, jnp.concatenate([k] * heads, axis=0) * hmask))
    return out


def weigh(scores, bias, masks):
    low = lax.broadcasted_iota(i32, (KEYS, 128), 1) < KEYS
    weights = []
    for w, s in enumerate(scores):
        parts = []
        for c in range(0, s.shape[1], 128):
            t = s[:, c : c + 128] + bias[:, c : c + 128]
            if masks is not None:
                t = jnp.where(masks[w], t, FAR)
            u = t.astype(bf16)
            first = jnp.max(jnp.where(low, u, bf16(-jnp.inf)), axis=-1, keepdims=True)
            second = jnp.max(jnp.where(low, bf16(-jnp.inf), u), axis=-1, keepdims=True)
            parts.append(jnp.exp2(t - jnp.where(low, first, second).astype(f32)))
        weights.append(jnp.concatenate(parts, axis=1).astype(bf16))
    return weights


def blend(weights, triple, hmask, heads):
    width = triple.shape[1] // 3
    outs = []
    for w, p in enumerate(weights):
        v = triple[w * KEYS : (w + 1) * KEYS, 2 * width :]
        o = dot(p, jnp.concatenate([jnp.concatenate([v] * heads, axis=0) * hmask, hmask], axis=1))
        outs.append((o[:, :width] / o[:, width:]).astype(bf16))
    return outs


def pipeline(tasks, depth):
    for task in tasks:
        for stage in task:
            if stage is not None:
                stage()


def fused(
    heads, group,
    x_h, lab_h, rel_h, gain_h, shift_h, qkvw_h, qkvb_h, table_h, projw_h, projb_h, fc1w_h, fc1b_h, fc2w_h, fc2b_h,
    o_ref,
    x_v, lab, rel, gain, shift, table, proj_b, fc2_b,
    qkv, proj, fc1, fc2, tab_all, qb_all, f1b_all, qb, f1b, bias, lab3, rt, ru,
    xq, nq, att, x1, below, yr, yt, yo,
    in_sem, ssend, srecv, wsend, wrecv, rsend, rrecv, lsend, lrecv, hsend, hrecv, esend, erecv,
    osend, orecv, fsend, frecv,
):
    rows, cols, width = x_v.shape
    nwin = cols // WIN
    chunks = nwin // group
    n = lax.axis_size("ch")
    nrow, ncol = lax.axis_size("row"), lax.axis_size("col")
    row, col, ch = lax.axis_index("row"), lax.axis_index("col"), lax.axis_index("ch")
    ring = row * n + ch
    total = nrow * n

    def at(dr, dc):
        p = lax.rem(ring + dr + total, total)
        return (p // n, lax.rem(col + dc + ncol, ncol), lax.rem(p, n))

    around = [(-1, 0), (0, -1), (-1, -1), (1, 0), (0, 1), (1, 1)]
    peers = [(row, col, lax.rem(ch + d, n)) for d in range(1, n)]
    mate = (row, col + 1 - 2 * lax.rem(col, 2), ch)
    core = lax.rem(col, 2)
    mesh_id = pl.DeviceIdType.MESH

    barrier = pltpu.get_barrier_semaphore()
    targets = [at(*d) for d in around] + peers + [mate]
    for t in targets:
        pl.semaphore_signal(barrier, inc=1, device_id=t, device_id_type=mesh_id)

    def remote(src, dst, ssem, rsem, to):
        return pltpu.make_async_remote_copy(
            src_ref=src, dst_ref=dst, send_sem=ssem, recv_sem=rsem, device_id=to, device_id_type=mesh_id
        )

    part, pw, fw, gw = width // n, projw_h.shape[1], fc1w_h.shape[2], fc2w_h.shape[1]

    def slots(b, owner, halves):
        out = []
        for i, size in enumerate((part, pw, width, gw)):
            start = owner * size if i != 2 else 0
            if halves[i]:
                size = size // 2
                start = start + core * size
            span = pl.ds(pl.multiple_of(start, 16), size)
            lanes = pl.ds(pl.multiple_of(owner * fw, 128), fw)
            out.append((
                lambda: qkv.at[b, :, span, :], lambda: proj.at[b, span, :],
                lambda: fc1.at[b, span, lanes], lambda: fc2.at[b, span, :],
            )[i]())
        return out

    loads = {}
    for i, (name, s, d) in enumerate([
        ("table", table_h, table), ("qb", qkvb_h, qb_all.at[ch]), ("f1b", fc1b_h, f1b_all.at[ch]),
        ("qkv", qkvw_h, qkv.at[:, :, pl.ds(pl.multiple_of(ch * part, 16), part), :]),
        ("proj", projw_h, proj.at[:, pl.ds(pl.multiple_of(ch * pw, 16), pw), :]),
        ("fc1", fc1w_h, fc1.at[:, :, pl.ds(pl.multiple_of(ch * fw, 128), fw)]),
        ("fc2", fc2w_h, fc2.at[:, pl.ds(pl.multiple_of(ch * gw, 16), gw), :]),
        ("lab", lab_h, lab), ("x", x_h, x_v), ("gain", gain_h, gain), ("shift", shift_h, shift),
        ("rel", rel_h, rel), ("proj_b", projb_h, proj_b), ("fc2_b", fc2b_h, fc2_b),
    ]):
        loads[name] = pltpu.make_async_copy(s, d, in_sem.at[i])
        loads[name].start()
    tab_all[ch, :, :, :] = jnp.zeros(tab_all.shape[1:], f32)
    loads["table"].wait()
    tab_all[ch, :, : table.shape[1], : table.shape[2]] = table[...]
    pl.semaphore_wait(barrier, len(targets))

    split = {0: (False, True, True, True), 1: (True, True, True, True)}
    direct, relays, smalls = {}, {}, []
    for d in range(1, n):
        to, owner = peers[d - 1], lax.rem(ch - d + n, n)
        for b in range(BLOCKS):
            for i, s in enumerate(slots(b, ch, split[b])):
                direct[d, b, i] = remote(s, s, wsend.at[d - 1, b, i], wrecv.at[d - 1, b, i], to)
            for i, s in enumerate(slots(b, owner, split[b])):
                if split[b][i]:
                    relays[d, b, i] = remote(s, s, rsend.at[d - 1, b, i], rrecv.at[d - 1, b, i], mate)
        for i, ref in enumerate([tab_all, qb_all, f1b_all]):
            smalls.append(remote(ref.at[ch], ref.at[ch], ssend.at[d - 1, i], srecv.at[d - 1, i], to))
    loads["qkv"].wait()
    for d in range(1, n):
        direct[d, 0, 0].start()
    loads["qb"].wait()
    loads["f1b"].wait()
    for c in smalls:
        c.start()
    for name in ("proj", "fc1", "fc2", "lab"):
        loads[name].wait()
    labels = []
    for i, d in enumerate(around[:3]):
        labels.append(remote(lab, lab3.at[i], lsend.at[i], lrecv.at[i], at(*d)))
        labels[-1].start()
    for b in range(BLOCKS):
        for d in range(1, n):
            for i in range(b == 0, 4):
                direct[d, b, i].start()

    for name in ("x", "gain", "shift", "rel", "proj_b", "fc2_b"):
        loads[name].wait()

    def here(k, more=0):
        return pl.ds(k * group, group + more)

    def prepare(k, _):
        t = quads(x_v[:, pl.ds(pl.multiple_of(k * group * WIN, WIN), group * WIN), :].astype(f32))
        xq[here(k)] = t.astype(bf16).reshape(group, KEYS, width)
        nq[here(k)] = layer_norm(t, gain[0, 0:1], shift[0, 0:1]).reshape(group, KEYS, width)
        return 0

    lax.fori_loop(0, chunks, prepare, 0)

    idx = quads(jnp.concatenate([rel[...]] * 2, axis=1).reshape(WIN, WIN, 128))
    lane = lax.broadcasted_iota(i32, (KEYS, 128), 1)
    a, c = place_of(lane & (KEYS - 1))
    idx = jnp.take_along_axis(idx, (lane & KEYS) + a * WIN + c, axis=1, mode="promise_in_bounds")
    for c in smalls:
        c.wait_recv()
    scale = (width // heads) ** (-0.5) * LOG2E
    for j in range(n):
        for b in range(BLOCKS):
            for m in range(3):
                qb[b, :, m * width + j * part : m * width + (j + 1) * part] = qb_all[j, m, b : b + 1, :]
            f1b[b, :, j * fw : (j + 1) * fw] = f1b_all[j, b : b + 1, :]
    local_heads = table.shape[1]
    for b in range(BLOCKS):
        for t in range(heads // 2):
            out = []
            for h in (2 * t, 2 * t + 1):
                entry = tab_all[h // local_heads, b, h % local_heads : h % local_heads + 1, :]
                got = None
                for c in range(0, entry.shape[1], 128):
                    piece = jnp.broadcast_to(entry[:, c : c + 128], idx.shape)
                    piece = jnp.take_along_axis(piece, idx & 127, axis=1, mode="promise_in_bounds")
                    got = piece if got is None else jnp.where(idx >= c, piece, got)
                out.append(got)
            bias[b, :, t * 128 : (t + 1) * 128] = jnp.where(lane < KEYS, out[0], out[1]) * LOG2E

    hmask = head_mask(heads, KEYS, width)
    lanes3 = lax.broadcasted_iota(i32, (1, 3 * width), 1)
    mult = jnp.where(lanes3 < width, scale, 1.0)

    def project(normed, b):
        return ((dot_t(normed, rows_of(qkv[b])) + qb[b]) * mult).astype(bf16)

    def regions():
        for c in labels:
            c.wait_recv()
        kind = jnp.concatenate([lab[SHIFT:], lab3[0, :SHIFT]], axis=0).astype(f32)
        kind = pltpu.roll(kind, cols - SHIFT, 1)
        wrap = jnp.concatenate([lab3[1, SHIFT:, :128], lab3[2, :SHIFT, :128]], axis=0).astype(f32)
        wrap = jnp.concatenate([jnp.zeros((rows, cols - 128), f32), pltpu.roll(wrap, 128 - SHIFT, 1)], axis=1)
        i = lax.broadcasted_iota(i32, (rows, cols), 0)
        j = lax.broadcasted_iota(i32, (rows, cols), 1)
        def flag(where, when):
            return jnp.where(where, when.astype(f32), 0.0)
        kind = jnp.where(j >= cols - SHIFT, wrap, kind) * 4.0
        kind = kind + flag(i >= SHIFT, ring == total - 1) * 2.0 + flag(j >= cols - SHIFT, col == ncol - 1)
        lane8 = lax.broadcasted_iota(i32, (rows, 128), 1)
        per = 128 // WIN
        stack = []
        for c in range(WIN):
            got = None
            for p in range(0, cols, 128):
                piece = jnp.take_along_axis(
                    kind[:, p : p + 128], (lane8 & (per - 1)) * WIN + c, axis=1, mode="promise_in_bounds"
                )
                got = piece if got is None else jnp.where(lane8 >= p // WIN, piece, got)
            stack.append(got)
        stack = jnp.concatenate(stack, axis=0).astype(bf16)
        a, c = place_of(lax.broadcasted_iota(i32, (128, KEYS), 0) & (KEYS - 1))
        pick = (c * WIN + a == lax.broadcasted_iota(i32, (128, KEYS), 1)).astype(f32).astype(bf16)
        kinds = dot(pick, stack)
        ru[...] = kinds.T
        for j in range(nwin):
            rt[j] = jnp.broadcast_to(kinds[:KEYS, j : j + 1], (KEYS, 128))

    def mix(x, attended, b):
        middle = (x + dot(attended, proj[b]) + proj_b[b : b + 1]).astype(bf16).astype(f32)
        return middle, layer_norm(middle, gain[b, 1:2], shift[b, 1:2])

    def feed(middle, normed, b):
        inner = (dot(normed, fc1[b]) + f1b[b]).astype(bf16)
        hidden = inner * (lax.erf(inner * bf16(0.5 ** 0.5)) + bf16(1.0))
        outer = dot(hidden, fc2[b] * bf16(0.5))
        return (middle + outer + fc2_b[b : b + 1]).astype(bf16)

    def halo(k):
        return remote(x1.at[here(k), : 2 * PART, :], below.at[here(k)], hsend.at[k], hrecv.at[k], at(-1, 0))

    edges = [
        remote(x1.at[0, 2 * PART : 3 * PART], x1.at[nwin, 2 * PART : 3 * PART], esend.at[0], erecv.at[0], at(0, -1)),
        remote(x1.at[0, :PART], below.at[nwin, :PART], esend.at[1], erecv.at[1], at(-1, -1)),
    ]

    def back(k):
        return remote(
            yr.at[here(k)], yt.at[pl.ds(k * group + 1, group)], osend.at[k], orecv.at[k], at(1, 0)
        )

    fringe = [
        remote(yo.at[nwin, PART :], yo.at[0, PART :], fsend.at[0], frecv.at[0], at(0, 1)),
        remote(yr.at[nwin - 1, PART :], yt.at[0, PART :], fsend.at[1], frecv.at[1], at(1, 1)),
    ]

    def bring(b):
        for d in range(1, n):
            for i in range(4):
                direct[d, b, i].wait_recv()
                if (d, b, i) in relays:
                    relays[d, b, i].start()

    def settle(b):
        for d in range(1, n):
            for i in range(4):
                if (d, b, i) in relays:
                    relays[d, b, i].wait_recv()

    def block0(k):
        st = {}

        def score():
            st["triple"] = project(rows_of(nq[here(k)]), 0)
            st["scores"] = scores_of(st["triple"], hmask, heads)

        def soften():
            st["att"] = blend(weigh(st["scores"], bias[0], None), st["triple"], hmask, heads)

        def middle():
            if k == last:
                settle(0)
            st["mid"] = mix(rows_of(xq[here(k)]).astype(f32), jnp.concatenate(st["att"], axis=0), 0)

        def close():
            x1[here(k)] = feed(*st["mid"], 0).reshape(group, KEYS, width)
            halo(k).start()
            if k == 0:
                for c in edges:
                    c.start()

        return [score, soften, middle, close]

    def own_half(k):
        out = []
        for g in range(k * group, (k + 1) * group):
            out += [x1[g, 3 * PART :], x1[g + 1, 2 * PART : 3 * PART]]
        return out

    def far_half(k):
        out = []
        for g in range(k * group, (k + 1) * group):
            out += [below[g, PART :], below[g + 1, :PART]]
        return out

    def block1(k):
        st = {}

        def score():
            for h in {last - 1: (last, last - 1), last: ()}.get(k, (k,)):
                halo(h).wait_recv()
            if k == last:
                for c in edges:
                    c.wait_recv()
            mine, other = own_half(k), far_half(k)
            toks = []
            for g in range(group):
                toks += mine[2 * g : 2 * g + 2] + other[2 * g : 2 * g + 2]
            toks = jnp.concatenate(toks, axis=0).astype(f32)
            st["triple"] = project(layer_norm(toks, gain[1, 0:1], shift[1, 0:1]), 1)
            st["scores"] = scores_of(st["triple"], hmask, heads)

        def soften():
            masks = [rt[g] == ru[g : g + 1, :] for g in range(k * group, (k + 1) * group)]
            outs = blend(weigh(st["scores"], bias[1], masks), st["triple"], hmask, heads)
            st["att"] = [o[2 * PART :] for o in outs]
            for g, o in enumerate(outs):
                att[k * group + g] = o[: 2 * PART]

        def middle():
            x = jnp.concatenate(far_half(k), axis=0).astype(f32)
            st["mid"] = mix(x, jnp.concatenate(st["att"], axis=0), 1)

        def close():
            yr[here(k)] = feed(*st["mid"], 1).reshape(group, 2 * PART, width)
            back(k).start()
            if k == last:
                fringe[1].start()

        return [score, soften, middle, close]

    def own(ks):
        st = {}

        def middle():
            x = jnp.concatenate(sum([own_half(k) for k in ks], []), axis=0).astype(f32)
            y = jnp.concatenate([rows_of(att[here(k)]) for k in ks], axis=0)
            st["mid"] = mix(x, y, 1)

        def close():
            y = feed(*st["mid"], 1).reshape(len(ks), group, 2 * PART, width)
            for i, k in enumerate(ks):
                yo[pl.ds(k * group + 1, group)] = y[i]
            if last in ks:
                fringe[0].start()

        return [None, None, middle, close]

    last = chunks - 1
    bring(0)
    pipeline([block0(k) for k in range(last, -1, -1)], 4)
    bring(1)
    regions()
    settle(1)
    order = list(range(last - 1, -1, -1)) + [last]
    owns = [own(order[::-1][i : i + 2]) for i in range(0, chunks, 2)]
    pipeline([block1(k) for k in order] + owns, 4)

    def place(src, base):
        v = src[...].astype(f32)
        for i in range(2):
            left, right = v[:nwin, PART + i * WIN : PART + (i + 1) * WIN], v[1:, i * WIN : (i + 1) * WIN]
            for r, y in enumerate(swap_halves(left, right)):
                o_ref[base + 2 * i + r] = y.reshape(cols, width).astype(bf16)

    fringe[0].wait_recv()
    place(yo, SHIFT)
    for k in range(chunks):
        back(k).wait_recv()
    fringe[1].wait_recv()
    place(yt, 0)
    for c in labels + smalls + edges + fringe + list(direct.values()) + list(relays.values()):
        c.wait_send()
    for k in range(chunks):
        halo(k).wait_send()
        back(k).wait_send()


def on_device(*args):
    x = args[0]
    rows, cols, width = x.shape
    n = lax.axis_size("ch")
    heads = args[7].shape[2] * n
    args = list(args)
    args[5] = args[5].swapaxes(2, 3)
    args[6] = args[6].swapaxes(0, 1)
    args[7] = args[7].swapaxes(1, 2)
    hidden = args[10].shape[2] * n
    nwin = cols // WIN
    group = max(d for d in range(1, MOST + 1) if nwin % d == 0)
    chunks = nwin // group
    assert rows == WIN and heads % 2 == 0 and chunks > 1
    dma = pltpu.SemaphoreType.DMA
    vm = pltpu.VMEM
    entries = args[7].shape[2] + -args[7].shape[2] % 128
    scratch = [
        vm(x.shape, bf16), vm((rows, cols), i32), vm(args[2].shape, i32), vm(args[3].shape, f32),
        vm(args[4].shape, f32), vm(args[7].shape, f32), vm(args[9].shape, f32), vm(args[13].shape, f32),
        vm((BLOCKS, 3, width, width), bf16), vm((BLOCKS, width, width), bf16),
        vm((BLOCKS, width, hidden), bf16), vm((BLOCKS, hidden, width), bf16),
        vm((n, BLOCKS, 8, entries), f32), vm((n,) + args[6].shape, f32), vm((n,) + args[11].shape, f32),
        vm((BLOCKS, 1, 3 * width), f32), vm((BLOCKS, 1, hidden), f32), vm((BLOCKS, KEYS, heads * KEYS), f32),
        vm((3, rows, cols), i32), vm((nwin, KEYS, 128), f32), vm((128, 128), f32),
        vm((nwin, KEYS, width), bf16), vm((nwin, KEYS, width), bf16), vm((nwin, 2 * PART, width), bf16),
        vm((nwin + 1, KEYS, width), bf16), vm((nwin + 1, 2 * PART, width), bf16),
        vm((nwin, 2 * PART, width), bf16), vm((nwin + 1, 2 * PART, width), bf16),
        vm((nwin + 1, 2 * PART, width), bf16),
        dma((14,)), dma((n - 1, 3)), dma((n - 1, 3)), dma((n - 1, BLOCKS, 4)), dma((n - 1, BLOCKS, 4)),
        dma((n - 1, BLOCKS, 4)), dma((n - 1, BLOCKS, 4)), dma((3,)), dma((3,)),
        dma((chunks,)), dma((chunks,)), dma((2,)), dma((2,)),
        dma((chunks,)), dma((chunks,)), dma((2,)), dma((2,)),
    ]
    return pl.pallas_call(
        functools.partial(fused, heads, group),
        out_shape=vm(x.shape, bf16),
        in_specs=[pl.BlockSpec(memory_space=pl.ANY)] * len(args),
        out_specs=pl.BlockSpec(memory_space=vm),
        scratch_shapes=scratch,
        compiler_params=pltpu.CompilerParams(
            collective_id=0, has_side_effects=True, vmem_limit_bytes=56 * 1024 * 1024
        ),
        name="fused",
    )(*args)


def solution(mesh):
    in_specs = (
        P(("row", "ch"), "col", None), P(("row", "ch"), "col"), P(), P(), P(),
        P(None, None, None, "ch"), P(None, None, "ch"), P(None, None, "ch"), P(None, "ch", None), P(),
        P(None, None, "ch"), P(None, "ch"), P(None, "ch", None), P(),
    )
    out_specs = P(("row", "ch"), "col", None)
    return jax.shard_map(on_device, mesh=mesh, in_specs=in_specs, out_specs=out_specs, check_vma=False)
```

time: 39.7 us -> 32 us (0.81)
  Pallas kernels: 37.6 us -> 31 us
  local copies, waits for them, and re-layouts: 1.87 us -> 0.8 us
    pallas_call x1, Pallas kernels: 37.6 us -> 31 us  [on_device(): pl.pallas_call(functools.partial(fused, heads, group), out_shape=vm(x.sha...]
    unnamed x1, local copies, waits for them, and re-layouts: 1.87 us -> 0.8 us
where the time goes in v1:
time: 32 us; the launch traced here: 31.8 us
  Pallas kernels  31 us (97%)
  local copies, waits for them, and re-layouts  0.8 us (2%)
    pallas_call x1, Pallas kernels, on_device(): pl.pallas_call(functools.partial(fused, heads, group), out_shape=vm(x.sha...  31 us
    unnamed x1, local copies, waits for them, and re-layouts  0.8 us

profile of v1, /device:TPU:0, one launch (start us, length us, event | category | flops | bytes accessed | tf_op | source)
XLA Modules:
  0.0 31.8 jit_solution(11957252504715381070)
XLA Ops:
  0.0 31.0 %fused.1 = bf16[8,256,128]{2,1,0:T(8,128)(2,1)S(1)} custom-call(bf16[8,256,128]{2,1,0:T(8,128)(2,1)} %x_h.1, s32[8,256]{1,0:T(8,128)} %lab_h.1, s32[64,64]{1,0:T(8,128)} %rel_h.1, f32[2,2,128]{2,1,0:T(2,128)} %gain_h.1, f32[2,2,128]{2,1,0:T(2,128)} %shift_h.1, bf16[2,3,64,128]{3,2,1,0:T(8,128)(2,1)} %bitcast.3, f32[3,2,64]{2,1,0:T(2,128)} %bitcast.5, ...), custom_call_target="tpu_custom_call" | custom-call | tf_op jit(solution)/shard_map/fused/pallas_call | solution.py:491
  31.0 0.8 %copy.16 = bf16[8,256,128]{2,1,0:T(8,128)(2,1)} copy(bf16[8,256,128]{2,1,0:T(8,128)(2,1)S(1)} %fused.1) | data formatting | bytes 1048576

commit v2 on v1

--- a/solution.py
+++ b/solution.py
@@ -14,6 +14,7 @@
 FAR = -1e30
 LOG2E = 1.4426950408889634
 MOST = 8
+ORDER = ("middle", "score", "close", "soften")
 bf16 = jnp.bfloat16
 f32 = jnp.float32
 i32 = jnp.int32
@@ -69,17 +70,17 @@
     return (row == col).astype(f32).astype(bf16)
 
 
-def scores_of(triple, hmask, heads):
+def scores_of(triple, hmask, heads, rows):
     width = triple.shape[1] // 3
     out = []
     for w in range(0, triple.shape[0], KEYS):
-        q, k = triple[w : w + KEYS, :width], triple[w : w + KEYS, width : 2 * width]
+        q, k = triple[w : w + KEYS, :width][rows], triple[w : w + KEYS, width : 2 * width]
         out.append(dot_t(q, jnp.concatenate([k] * heads, axis=0) * hmask))
     return out
 
 
 def weigh(scores, bias, masks):
-    low = lax.broadcasted_iota(i32, (KEYS, 128), 1) < KEYS
+    low = lax.broadcasted_iota(i32, (bias.shape[0], 128), 1) < KEYS
     weights = []
     for w, s in enumerate(scores):
         parts = []
@@ -105,20 +106,22 @@
     return outs
 
 
-def pipeline(tasks, depth):
-    for task in tasks:
-        for stage in task:
-            if stage is not None:
-                stage()
+def overlap(now, before):
+    if now is not None:
+        now["wait"]()
+    for stage in ORDER:
+        task = now if stage in ("score", "soften") else before
+        if task is not None:
+            task[stage]()
 
 
 def fused(
     heads, group,
     x_h, lab_h, rel_h, gain_h, shift_h, qkvw_h, qkvb_h, table_h, projw_h, projb_h, fc1w_h, fc1b_h, fc2w_h, fc2b_h,
     o_ref,
-    x_v, lab, rel, gain, shift, table, proj_b, fc2_b,
+    x_v, lab, rel, gain, shift, proj_b, fc2_b,
     qkv, proj, fc1, fc2, tab_all, qb_all, f1b_all, qb, f1b, bias, lab3, rt, ru,
-    xq, nq, att, x1, below, yr, yt, yo,
+    xq, nq, tri, x1, below, yr, yt, yo,
     in_sem, ssend, srecv, wsend, wrecv, rsend, rrecv, lsend, lrecv, hsend, hrecv, esend, erecv,
     osend, orecv, fsend, frecv,
 ):
@@ -170,7 +173,7 @@
 
     loads = {}
     for i, (name, s, d) in enumerate([
-        ("table", table_h, table), ("qb", qkvb_h, qb_all.at[ch]), ("f1b", fc1b_h, f1b_all.at[ch]),
+        ("table", table_h, tab_all.at[ch]), ("qb", qkvb_h, qb_all.at[ch]), ("f1b", fc1b_h, f1b_all.at[ch]),
         ("qkv", qkvw_h, qkv.at[:, :, pl.ds(pl.multiple_of(ch * part, 16), part), :]),
         ("proj", projw_h, proj.at[:, pl.ds(pl.multiple_of(ch * pw, 16), pw), :]),
         ("fc1", fc1w_h, fc1.at[:, :, pl.ds(pl.multiple_of(ch * fw, 128), fw)]),
@@ -180,12 +183,9 @@
     ]):
         loads[name] = pltpu.make_async_copy(s, d, in_sem.at[i])
         loads[name].start()
-    tab_all[ch, :, :, :] = jnp.zeros(tab_all.shape[1:], f32)
-    loads["table"].wait()
-    tab_all[ch, :, : table.shape[1], : table.shape[2]] = table[...]
     pl.semaphore_wait(barrier, len(targets))
 
-    split = {0: (False, True, True, True), 1: (True, True, True, True)}
+    split = {0: (False, False, True, True), 1: (True, True, True, True)}
     direct, relays, smalls = {}, {}, []
     for d in range(1, n):
         to, owner = peers[d - 1], lax.rem(ch - d + n, n)
@@ -197,24 +197,19 @@
                     relays[d, b, i] = remote(s, s, rsend.at[d - 1, b, i], rrecv.at[d - 1, b, i], mate)
         for i, ref in enumerate([tab_all, qb_all, f1b_all]):
             smalls.append(remote(ref.at[ch], ref.at[ch], ssend.at[d - 1, i], srecv.at[d - 1, i], to))
-    loads["qkv"].wait()
-    for d in range(1, n):
-        direct[d, 0, 0].start()
-    loads["qb"].wait()
-    loads["f1b"].wait()
-    for c in smalls:
-        c.start()
-    for name in ("proj", "fc1", "fc2", "lab"):
-        loads[name].wait()
+    loads["lab"].wait()
     labels = []
     for i, d in enumerate(around[:3]):
         labels.append(remote(lab, lab3.at[i], lsend.at[i], lrecv.at[i], at(*d)))
         labels[-1].start()
+    for name in ("table", "qb", "f1b", "qkv", "proj", "fc1", "fc2"):
+        loads[name].wait()
+    for c in smalls:
+        c.start()
     for b in range(BLOCKS):
-        for d in range(1, n):
-            for i in range(b == 0, 4):
+        for i in range(4):
+            for d in range(1, n):
                 direct[d, b, i].start()
-
     for name in ("x", "gain", "shift", "rel", "proj_b", "fc2_b"):
         loads[name].wait()
 
@@ -241,15 +236,18 @@
             for m in range(3):
                 qb[b, :, m * width + j * part : m * width + (j + 1) * part] = qb_all[j, m, b : b + 1, :]
             f1b[b, :, j * fw : (j + 1) * fw] = f1b_all[j, b : b + 1, :]
-    local_heads = table.shape[1]
+    local_heads, entries = table_h.shape[1:]
     for b in range(BLOCKS):
         for t in range(heads // 2):
             out = []
             for h in (2 * t, 2 * t + 1):
                 entry = tab_all[h // local_heads, b, h % local_heads : h % local_heads + 1, :]
                 got = None
-                for c in range(0, entry.shape[1], 128):
-                    piece = jnp.broadcast_to(entry[:, c : c + 128], idx.shape)
+                for c in range(0, entries, 128):
+                    piece = entry[:, c : c + 128]
+                    if piece.shape[1] < 128:
+                        piece = jnp.concatenate([piece, jnp.zeros((1, 128 - piece.shape[1]), f32)], axis=1)
+                    piece = jnp.broadcast_to(piece, idx.shape)
                     piece = jnp.take_along_axis(piece, idx & 127, axis=1, mode="promise_in_bounds")
                     got = piece if got is None else jnp.where(idx >= c, piece, got)
                 out.append(got)
@@ -291,8 +289,7 @@
         pick = (c * WIN + a == lax.broadcasted_iota(i32, (128, KEYS), 1)).astype(f32).astype(bf16)
         kinds = dot(pick, stack)
         ru[...] = kinds.T
-        for j in range(nwin):
-            rt[j] = jnp.broadcast_to(kinds[:KEYS, j : j + 1], (KEYS, 128))
+        rt[...] = kinds[:KEYS]
 
     def mix(x, attended, b):
         middle = (x + dot(attended, proj[b]) + proj_b[b : b + 1]).astype(bf16).astype(f32)
@@ -312,9 +309,12 @@
         remote(x1.at[0, :PART], below.at[nwin, :PART], esend.at[1], erecv.at[1], at(-1, -1)),
     ]
 
-    def back(k):
+    spans = [(k * group, group - (k == chunks - 1)) for k in range(chunks)] + [(nwin - 1, 1)]
+
+    def back(i):
+        start, size = spans[i]
         return remote(
-            yr.at[here(k)], yt.at[pl.ds(k * group + 1, group)], osend.at[k], orecv.at[k], at(1, 0)
+            yr.at[pl.ds(start, size)], yt.at[pl.ds(start + 1, size)], osend.at[i], orecv.at[i], at(1, 0)
         )
 
     fringe = [
@@ -322,9 +322,9 @@
         remote(yr.at[nwin - 1, PART :], yt.at[0, PART :], fsend.at[1], frecv.at[1], at(1, 1)),
     ]
 
-    def bring(b):
-        for d in range(1, n):
-            for i in range(4):
+    def bring(b, pieces):
+        for i in pieces:
+            for d in range(1, n):
                 direct[d, b, i].wait_recv()
                 if (d, b, i) in relays:
                     relays[d, b, i].start()
@@ -338,16 +338,17 @@
     def block0(k):
         st = {}
 
+        def wait():
+            pass
+
         def score():
             st["triple"] = project(rows_of(nq[here(k)]), 0)
-            st["scores"] = scores_of(st["triple"], hmask, heads)
+            st["scores"] = scores_of(st["triple"], hmask, heads, slice(None))
 
         def soften():
             st["att"] = blend(weigh(st["scores"], bias[0], None), st["triple"], hmask, heads)
 
         def middle():
-            if k == last:
-                settle(0)
             st["mid"] = mix(rows_of(xq[here(k)]).astype(f32), jnp.concatenate(st["att"], axis=0), 0)
 
         def close():
@@ -357,82 +358,103 @@
                 for c in edges:
                     c.start()
 
-        return [score, soften, middle, close]
-
-    def own_half(k):
-        out = []
-        for g in range(k * group, (k + 1) * group):
-            out += [x1[g, 3 * PART :], x1[g + 1, 2 * PART : 3 * PART]]
-        return out
-
-    def far_half(k):
-        out = []
-        for g in range(k * group, (k + 1) * group):
-            out += [below[g, PART :], below[g + 1, :PART]]
-        return out
-
-    def block1(k):
+        return {"wait": wait, "score": score, "soften": soften, "middle": middle, "close": close}
+
+    def own_half(ws):
+        return sum([[x1[w, 3 * PART :], x1[w + 1, 2 * PART : 3 * PART]] for w in ws], [])
+
+    def far_half(ws):
+        return sum([[below[w, PART :], below[w + 1, :PART]] for w in ws], [])
+
+    near, far = slice(0, 2 * PART), slice(2 * PART, KEYS)
+
+    def masks(ws, part):
+        return [jnp.broadcast_to(rt[part, w : w + 1], (2 * PART, 128)) == ru[w : w + 1, :] for w in ws]
+
+    def split_rows(x):
+        return [x[i : i + 2 * PART] for i in range(0, x.shape[0], 2 * PART)]
+
+    def block1(ids, halos):
         st = {}
+        ws = [w for i in ids for w in range(spans[i][0], sum(spans[i]))]
+
+        def wait():
+            for c in halos:
+                c.wait_recv()
 
         def score():
-            for h in {last - 1: (last, last - 1), last: ()}.get(k, (k,)):
-                halo(h).wait_recv()
-            if k == last:
-                for c in edges:
-                    c.wait_recv()
-            mine, other = own_half(k), far_half(k)
+            mine, other = own_half(ws), far_half(ws)
             toks = []
-            for g in range(group):
-                toks += mine[2 * g : 2 * g + 2] + other[2 * g : 2 * g + 2]
+            for g in range(0, 2 * len(ws), 2):
+                toks += mine[g : g + 2] + other[g : g + 2]
             toks = jnp.concatenate(toks, axis=0).astype(f32)
             st["triple"] = project(layer_norm(toks, gain[1, 0:1], shift[1, 0:1]), 1)
-            st["scores"] = scores_of(st["triple"], hmask, heads)
+            for i, w in enumerate(ws):
+                tri[w] = st["triple"][i * KEYS : (i + 1) * KEYS]
+            st["scores"] = scores_of(st["triple"], hmask, heads, far)
 
         def soften():
-            masks = [rt[g] == ru[g : g + 1, :] for g in range(k * group, (k + 1) * group)]
-            outs = blend(weigh(st["scores"], bias[1], masks), st["triple"], hmask, heads)
-            st["att"] = [o[2 * PART :] for o in outs]
-            for g, o in enumerate(outs):
-                att[k * group + g] = o[: 2 * PART]
+            st["att"] = blend(weigh(st["scores"], bias[1, far, :], masks(ws, far)), st["triple"], hmask, heads)
 
         def middle():
-            x = jnp.concatenate(far_half(k), axis=0).astype(f32)
+            x = jnp.concatenate(far_half(ws), axis=0).astype(f32)
             st["mid"] = mix(x, jnp.concatenate(st["att"], axis=0), 1)
 
         def close():
-            yr[here(k)] = feed(*st["mid"], 1).reshape(group, 2 * PART, width)
-            back(k).start()
-            if k == last:
+            for w, y in zip(ws, split_rows(feed(*st["mid"], 1))):
+                yr[w] = y
+            for i in ids:
+                back(i).start()
+            if nwin - 1 in ws:
                 fringe[1].start()
 
-        return [score, soften, middle, close]
-
-    def own(ks):
+        return {"wait": wait, "score": score, "soften": soften, "middle": middle, "close": close}
+
+    def own(ws):
         st = {}
 
+        def wait():
+            pass
+
+        def score():
+            st["triple"] = jnp.concatenate([tri[w] for w in ws], axis=0)
+            st["scores"] = scores_of(st["triple"], hmask, heads, near)
+
+        def soften():
+            st["att"] = blend(weigh(st["scores"], bias[1, near, :], masks(ws, near)), st["triple"], hmask, heads)
+
         def middle():
-            x = jnp.concatenate(sum([own_half(k) for k in ks], []), axis=0).astype(f32)
-            y = jnp.concatenate([rows_of(att[here(k)]) for k in ks], axis=0)
-            st["mid"] = mix(x, y, 1)
+            x = jnp.concatenate(own_half(ws), axis=0).astype(f32)
+            st["mid"] = mix(x, jnp.concatenate(st["att"], axis=0), 1)
 
         def close():
-            y = feed(*st["mid"], 1).reshape(len(ks), group, 2 * PART, width)
-            for i, k in enumerate(ks):
-                yo[pl.ds(k * group + 1, group)] = y[i]
-            if last in ks:
+            for w, y in zip(ws, split_rows(feed(*st["mid"], 1))):
+                yo[w + 1] = y
+            if nwin - 1 in ws:
                 fringe[0].start()
 
-        return [None, None, middle, close]
+        return {"wait": wait, "score": score, "soften": soften, "middle": middle, "close": close}
 
     last = chunks - 1
-    bring(0)
-    pipeline([block0(k) for k in range(last, -1, -1)], 4)
-    bring(1)
+    first = [block0(k) for k in range(last, -1, -1)]
+    bring(0, (0,))
+    overlap(first[0], None)
+    bring(0, (1, 2, 3))
     regions()
+    first[0]["middle"]()
+    settle(0)
+    first[0]["close"]()
+    first[1]["score"]()
+    first[1]["soften"]()
+    bring(1, range(4))
+    for t in range(1, chunks):
+        overlap(first[t + 1] if t < last else None, first[t])
     settle(1)
-    order = list(range(last - 1, -1, -1)) + [last]
-    owns = [own(order[::-1][i : i + 2]) for i in range(0, chunks, 2)]
-    pipeline([block1(k) for k in order] + owns, 4)
+    second = [block1([k], [halo(k)]) for k in range(last, 0, -1)] + [block1([0, chunks], [halo(0)] + edges)]
+    half = nwin // 2
+    second += [own([nwin - 1] + list(range(half - 1))), own(list(range(half - 1, nwin - 1)))]
+    for t in range(len(second) + 1):
+        overlap(second[t] if t < len(second) else None, second[t - 1] if t > 0 else None)
 
     def place(src, base):
         v = src[...].astype(f32)
@@ -443,7 +465,7 @@
 
     fringe[0].wait_recv()
     place(yo, SHIFT)
-    for k in range(chunks):
+    for k in range(chunks + 1):
         back(k).wait_recv()
     fringe[1].wait_recv()
     place(yt, 0)
@@ -451,6 +473,7 @@
         c.wait_send()
     for k in range(chunks):
         halo(k).wait_send()
+    for k in range(chunks + 1):
         back(k).wait_send()
 
 
@@ -470,23 +493,22 @@
     assert rows == WIN and heads % 2 == 0 and chunks > 1
     dma = pltpu.SemaphoreType.DMA
     vm = pltpu.VMEM
-    entries = args[7].shape[2] + -args[7].shape[2] % 128
     scratch = [
         vm(x.shape, bf16), vm((rows, cols), i32), vm(args[2].shape, i32), vm(args[3].shape, f32),
-        vm(args[4].shape, f32), vm(args[7].shape, f32), vm(args[9].shape, f32), vm(args[13].shape, f32),
+        vm(args[4].shape, f32), vm(args[9].shape, f32), vm(args[13].shape, f32),
         vm((BLOCKS, 3, width, width), bf16), vm((BLOCKS, width, width), bf16),
         vm((BLOCKS, width, hidden), bf16), vm((BLOCKS, hidden, width), bf16),
-        vm((n, BLOCKS, 8, entries), f32), vm((n,) + args[6].shape, f32), vm((n,) + args[11].shape, f32),
+        vm((n,) + args[7].shape, f32), vm((n,) + args[6].shape, f32), vm((n,) + args[11].shape, f32),
         vm((BLOCKS, 1, 3 * width), f32), vm((BLOCKS, 1, hidden), f32), vm((BLOCKS, KEYS, heads * KEYS), f32),
-        vm((3, rows, cols), i32), vm((nwin, KEYS, 128), f32), vm((128, 128), f32),
-        vm((nwin, KEYS, width), bf16), vm((nwin, KEYS, width), bf16), vm((nwin, 2 * PART, width), bf16),
+        vm((3, rows, cols), i32), vm((KEYS, 128), f32), vm((128, 128), f32),
+        vm((nwin, KEYS, width), bf16), vm((nwin, KEYS, width), bf16), vm((nwin, KEYS, 3 * width), bf16),
         vm((nwin + 1, KEYS, width), bf16), vm((nwin + 1, 2 * PART, width), bf16),
         vm((nwin, 2 * PART, width), bf16), vm((nwin + 1, 2 * PART, width), bf16),
         vm((nwin + 1, 2 * PART, width), bf16),
         dma((14,)), dma((n - 1, 3)), dma((n - 1, 3)), dma((n - 1, BLOCKS, 4)), dma((n - 1, BLOCKS, 4)),
         dma((n - 1, BLOCKS, 4)), dma((n - 1, BLOCKS, 4)), dma((3,)), dma((3,)),
         dma((chunks,)), dma((chunks,)), dma((2,)), dma((2,)),
-        dma((chunks,)), dma((chunks,)), dma((2,)), dma((2,)),
+        dma((chunks + 1,)), dma((chunks + 1,)), dma((2,)), dma((2,)),
     ]
     return pl.pallas_call(
         functools.partial(fused, heads, group),

time: 32 us -> 30.1 us (0.941)
  Pallas kernels: 31 us -> 29.1 us
    pallas_call x1, Pallas kernels: 31 us -> 29.1 us  [on_device(): pl.pallas_call(functools.partial(fused, heads, group), out_shape=vm(x.sha...]
where the time goes in v2:
time: 30.1 us; the launch traced here: 29.9 us
  Pallas kernels  29.1 us (97%)
  local copies, waits for them, and re-layouts  0.8 us (3%)
    pallas_call x1, Pallas kernels, on_device(): pl.pallas_call(functools.partial(fused, heads, group), out_shape=vm(x.sha...  29.1 us
    unnamed x1, local copies, waits for them, and re-layouts  0.8 us

profile of v2, /device:TPU:0, one launch (start us, length us, event | category | flops | bytes accessed | tf_op | source)
XLA Modules:
  0.0 29.9 jit_solution(3437405935384412503)
XLA Ops:
  0.0 29.1 %fused.1 = bf16[8,256,128]{2,1,0:T(8,128)(2,1)S(1)} custom-call(bf16[8,256,128]{2,1,0:T(8,128)(2,1)} %x_h.1, s32[8,256]{1,0:T(8,128)} %lab_h.1, s32[64,64]{1,0:T(8,128)} %rel_h.1, f32[2,2,128]{2,1,0:T(2,128)} %gain_h.1, f32[2,2,128]{2,1,0:T(2,128)} %shift_h.1, bf16[2,3,64,128]{3,2,1,0:T(8,128)(2,1)} %bitcast.3, f32[3,2,64]{2,1,0:T(2,128)} %bitcast.5, ...), custom_call_target="tpu_custom_call" | custom-call | tf_op jit(solution)/shard_map/fused/pallas_call | solution.py:513
  29.2 0.8 %copy.16 = bf16[8,256,128]{2,1,0:T(8,128)(2,1)} copy(bf16[8,256,128]{2,1,0:T(8,128)(2,1)S(1)} %fused.1) | data formatting | bytes 1048576

commit v3 on v2

--- a/solution.py
+++ b/solution.py
@@ -14,6 +14,7 @@
 FAR = -1e30
 LOG2E = 1.4426950408889634
 MOST = 8
+WHOLE = ((0, 1),)
 ORDER = ("middle", "score", "close", "soften")
 bf16 = jnp.bfloat16
 f32 = jnp.float32
@@ -70,11 +71,11 @@
     return (row == col).astype(f32).astype(bf16)
 
 
-def scores_of(triple, hmask, heads, rows):
+def scores_of(triple, hmask, heads):
     width = triple.shape[1] // 3
     out = []
     for w in range(0, triple.shape[0], KEYS):
-        q, k = triple[w : w + KEYS, :width][rows], triple[w : w + KEYS, width : 2 * width]
+        q, k = triple[w : w + KEYS, :width], triple[w : w + KEYS, width : 2 * width]
         out.append(dot_t(q, jnp.concatenate([k] * heads, axis=0) * hmask))
     return out
 
@@ -121,9 +122,9 @@
     o_ref,
     x_v, lab, rel, gain, shift, proj_b, fc2_b,
     qkv, proj, fc1, fc2, tab_all, qb_all, f1b_all, qb, f1b, bias, lab3, rt, ru,
-    xq, nq, tri, x1, below, yr, yt, yo,
+    xq, nq, att, x1, above, yr, yt, yo,
     in_sem, ssend, srecv, wsend, wrecv, rsend, rrecv, lsend, lrecv, hsend, hrecv, esend, erecv,
-    osend, orecv, fsend, frecv,
+    osend, orecv, fsend, frecv, ready,
 ):
     rows, cols, width = x_v.shape
     nwin = cols // WIN
@@ -138,14 +139,14 @@
         p = lax.rem(ring + dr + total, total)
         return (p // n, lax.rem(col + dc + ncol, ncol), lax.rem(p, n))
 
-    around = [(-1, 0), (0, -1), (-1, -1), (1, 0), (0, 1), (1, 1)]
+    around = [(1, 0), (0, -1), (1, -1), (-1, 0), (0, 1), (-1, 1)]
     peers = [(row, col, lax.rem(ch + d, n)) for d in range(1, n)]
     mate = (row, col + 1 - 2 * lax.rem(col, 2), ch)
     core = lax.rem(col, 2)
     mesh_id = pl.DeviceIdType.MESH
 
     barrier = pltpu.get_barrier_semaphore()
-    targets = [at(*d) for d in around] + peers + [mate]
+    targets = [at(*d) for d in around[3:]] + peers + [mate]
     for t in targets:
         pl.semaphore_signal(barrier, inc=1, device_id=t, device_id_type=mesh_id)
 
@@ -156,13 +157,13 @@
 
     part, pw, fw, gw = width // n, projw_h.shape[1], fc1w_h.shape[2], fc2w_h.shape[1]
 
-    def slots(b, owner, halves):
+    def slots(b, owner, share, count):
         out = []
         for i, size in enumerate((part, pw, width, gw)):
             start = owner * size if i != 2 else 0
-            if halves[i]:
-                size = size // 2
-                start = start + core * size
+            if (b, i) not in WHOLE:
+                size = size // count
+                start = start + share * size
             span = pl.ds(pl.multiple_of(start, 16), size)
             lanes = pl.ds(pl.multiple_of(owner * fw, 128), fw)
             out.append((
@@ -184,17 +185,22 @@
         loads[name] = pltpu.make_async_copy(s, d, in_sem.at[i])
         loads[name].start()
     pl.semaphore_wait(barrier, len(targets))
-
-    split = {0: (False, False, True, True), 1: (True, True, True, True)}
+    for d in (around[0], around[2]):
+        pl.semaphore_signal(ready, inc=1, device_id=at(*d), device_id_type=mesh_id)
+
+    shares = {b: (core, 2, [mate]) for b in range(BLOCKS)}
     direct, relays, smalls = {}, {}, []
     for d in range(1, n):
         to, owner = peers[d - 1], lax.rem(ch - d + n, n)
         for b in range(BLOCKS):
-            for i, s in enumerate(slots(b, ch, split[b])):
+            share, count, others = shares[b]
+            for i, s in enumerate(slots(b, ch, share, count)):
                 direct[d, b, i] = remote(s, s, wsend.at[d - 1, b, i], wrecv.at[d - 1, b, i], to)
-            for i, s in enumerate(slots(b, owner, split[b])):
-                if split[b][i]:
-                    relays[d, b, i] = remote(s, s, rsend.at[d - 1, b, i], rrecv.at[d - 1, b, i], mate)
+            for e, other in enumerate(others):
+                for i, s in enumerate(slots(b, owner, share, count)):
+                    if (b, i) not in WHOLE:
+                        r = b + e
+                        relays[d, b, i, e] = remote(s, s, rsend.at[d - 1, r, i], rrecv.at[d - 1, r, i], other)
         for i, ref in enumerate([tab_all, qb_all, f1b_all]):
             smalls.append(remote(ref.at[ch], ref.at[ch], ssend.at[d - 1, i], srecv.at[d - 1, i], to))
     loads["lab"].wait()
@@ -263,16 +269,16 @@
     def regions():
         for c in labels:
             c.wait_recv()
-        kind = jnp.concatenate([lab[SHIFT:], lab3[0, :SHIFT]], axis=0).astype(f32)
+        kind = jnp.concatenate([lab3[0, SHIFT:], lab[:SHIFT]], axis=0).astype(f32)
         kind = pltpu.roll(kind, cols - SHIFT, 1)
-        wrap = jnp.concatenate([lab3[1, SHIFT:, :128], lab3[2, :SHIFT, :128]], axis=0).astype(f32)
+        wrap = jnp.concatenate([lab3[2, SHIFT:, :128], lab3[1, :SHIFT, :128]], axis=0).astype(f32)
         wrap = jnp.concatenate([jnp.zeros((rows, cols - 128), f32), pltpu.roll(wrap, 128 - SHIFT, 1)], axis=1)
         i = lax.broadcasted_iota(i32, (rows, cols), 0)
         j = lax.broadcasted_iota(i32, (rows, cols), 1)
         def flag(where, when):
             return jnp.where(where, when.astype(f32), 0.0)
         kind = jnp.where(j >= cols - SHIFT, wrap, kind) * 4.0
-        kind = kind + flag(i >= SHIFT, ring == total - 1) * 2.0 + flag(j >= cols - SHIFT, col == ncol - 1)
+        kind = kind + flag(i >= SHIFT, ring == 0) * 2.0 + flag(j >= cols - SHIFT, col == ncol - 1)
         lane8 = lax.broadcasted_iota(i32, (rows, 128), 1)
         per = 128 // WIN
         stack = []
@@ -301,82 +307,104 @@
         outer = dot(hidden, fc2[b] * bf16(0.5))
         return (middle + outer + fc2_b[b : b + 1]).astype(bf16)
 
-    def halo(k):
-        return remote(x1.at[here(k), : 2 * PART, :], below.at[here(k)], hsend.at[k], hrecv.at[k], at(-1, 0))
+    cut = group // 2
+    final = nwin - group
+    heads_of = [(0, 1), (final, cut), (final + cut, group - cut)]
+    heads_of += [(k * group, group) for k in range(chunks - 2, 0, -1)] + [(1, group - 1)]
+
+    def halo(i):
+        start, size = heads_of[i]
+        span = pl.ds(start, size)
+        return remote(x1.at[span, 2 * PART :, :], above.at[span], hsend.at[i], hrecv.at[i], at(1, 0))
 
     edges = [
-        remote(x1.at[0, 2 * PART : 3 * PART], x1.at[nwin, 2 * PART : 3 * PART], esend.at[0], erecv.at[0], at(0, -1)),
-        remote(x1.at[0, :PART], below.at[nwin, :PART], esend.at[1], erecv.at[1], at(-1, -1)),
+        remote(x1.at[0, :PART], x1.at[nwin, :PART], esend.at[0], erecv.at[0], at(0, -1)),
+        remote(x1.at[0, 2 * PART : 3 * PART], above.at[nwin, :PART], esend.at[1], erecv.at[1], at(1, -1)),
     ]
 
-    spans = [(k * group, group - (k == chunks - 1)) for k in range(chunks)] + [(nwin - 1, 1)]
+    spans = [(k * group, group) for k in range(chunks - 1, 0, -1)] + [(0, cut), (cut, group - cut)]
 
     def back(i):
         start, size = spans[i]
         return remote(
-            yr.at[pl.ds(start, size)], yt.at[pl.ds(start + 1, size)], osend.at[i], orecv.at[i], at(1, 0)
+            yr.at[pl.ds(start, size)], yt.at[pl.ds(start + 1, size)], osend.at[i], orecv.at[i], at(-1, 0)
         )
 
     fringe = [
         remote(yo.at[nwin, PART :], yo.at[0, PART :], fsend.at[0], frecv.at[0], at(0, 1)),
-        remote(yr.at[nwin - 1, PART :], yt.at[0, PART :], fsend.at[1], frecv.at[1], at(1, 1)),
+        remote(yr.at[nwin - 1, PART :], yt.at[0, PART :], fsend.at[1], frecv.at[1], at(-1, 1)),
     ]
 
     def bring(b, pieces):
         for i in pieces:
             for d in range(1, n):
                 direct[d, b, i].wait_recv()
-                if (d, b, i) in relays:
-                    relays[d, b, i].start()
-
-    def settle(b):
-        for d in range(1, n):
-            for i in range(4):
-                if (d, b, i) in relays:
-                    relays[d, b, i].wait_recv()
-
-    def block0(k):
+                for e in range(len(shares[b][2])):
+                    if (d, b, i, e) in relays:
+                        relays[d, b, i, e].start()
+
+    def settle(b, pieces):
+        for (_, r, i, _), c in relays.items():
+            if r == b and i in pieces:
+                c.wait_recv()
+
+    def windows(pairs, ids):
+        return sum([list(range(pairs[i][0], sum(pairs[i]))) for i in ids], [])
+
+    def gather(ref, ws):
+        return jnp.concatenate([ref[w] for w in ws], axis=0)
+
+    def block0(parts):
         st = {}
+        parts = [(windows(heads_of, ids), ids) for ids in parts]
+        ws = sum([p for p, _ in parts], [])
 
         def wait():
             pass
 
         def score():
-            st["triple"] = project(rows_of(nq[here(k)]), 0)
-            st["scores"] = scores_of(st["triple"], hmask, heads, slice(None))
+            st["triple"] = project(gather(nq, ws), 0)
+            st["scores"] = scores_of(st["triple"], hmask, heads)
 
         def soften():
             st["att"] = blend(weigh(st["scores"], bias[0], None), st["triple"], hmask, heads)
 
         def middle():
-            st["mid"] = mix(rows_of(xq[here(k)]).astype(f32), jnp.concatenate(st["att"], axis=0), 0)
+            st["mid"] = mix(gather(xq, ws).astype(f32), jnp.concatenate(st["att"], axis=0), 0)
 
         def close():
-            x1[here(k)] = feed(*st["mid"], 0).reshape(group, KEYS, width)
-            halo(k).start()
-            if k == 0:
-                for c in edges:
-                    c.start()
+            mid, normed = st["mid"]
+            start = 0
+            for p, ids in parts:
+                end = start + len(p) * KEYS
+                y = feed(mid[start:end], normed[start:end], 0)
+                for g, w in enumerate(p):
+                    x1[w] = y[g * KEYS : (g + 1) * KEYS]
+                start = end
+                for i in ids:
+                    halo(i).start()
+                if 0 in p:
+                    for c in edges:
+                        c.start()
 
         return {"wait": wait, "score": score, "soften": soften, "middle": middle, "close": close}
 
     def own_half(ws):
-        return sum([[x1[w, 3 * PART :], x1[w + 1, 2 * PART : 3 * PART]] for w in ws], [])
+        return sum([[x1[w, PART : 2 * PART], x1[w + 1, :PART]] for w in ws], [])
 
     def far_half(ws):
-        return sum([[below[w, PART :], below[w + 1, :PART]] for w in ws], [])
-
-    near, far = slice(0, 2 * PART), slice(2 * PART, KEYS)
-
-    def masks(ws, part):
-        return [jnp.broadcast_to(rt[part, w : w + 1], (2 * PART, 128)) == ru[w : w + 1, :] for w in ws]
+        return sum([[above[w, PART :], above[w + 1, :PART]] for w in ws], [])
+
+    def masks(ws):
+        return [jnp.broadcast_to(rt[:, w : w + 1], (KEYS, 128)) == ru[w : w + 1, :] for w in ws]
 
     def split_rows(x):
         return [x[i : i + 2 * PART] for i in range(0, x.shape[0], 2 * PART)]
 
-    def block1(ids, halos):
+    def block1(parts, halos):
         st = {}
-        ws = [w for i in ids for w in range(spans[i][0], sum(spans[i]))]
+        parts = [(windows(spans, ids), ids) for ids in parts]
+        ws = sum([p for p, _ in parts], [])
 
         def wait():
             for c in halos:
@@ -386,75 +414,74 @@
             mine, other = own_half(ws), far_half(ws)
             toks = []
             for g in range(0, 2 * len(ws), 2):
-                toks += mine[g : g + 2] + other[g : g + 2]
+                toks += other[g : g + 2] + mine[g : g + 2]
             toks = jnp.concatenate(toks, axis=0).astype(f32)
             st["triple"] = project(layer_norm(toks, gain[1, 0:1], shift[1, 0:1]), 1)
-            for i, w in enumerate(ws):
-                tri[w] = st["triple"][i * KEYS : (i + 1) * KEYS]
-            st["scores"] = scores_of(st["triple"], hmask, heads, far)
+            st["scores"] = scores_of(st["triple"], hmask, heads)
 
         def soften():
-            st["att"] = blend(weigh(st["scores"], bias[1, far, :], masks(ws, far)), st["triple"], hmask, heads)
+            outs = blend(weigh(st["scores"], bias[1], masks(ws)), st["triple"], hmask, heads)
+            st["att"] = [o[: 2 * PART] for o in outs]
+            for w, o in zip(ws, outs):
+                att[w] = o[2 * PART :]
 
         def middle():
-            x = jnp.concatenate(far_half(ws), axis=0).astype(f32)
-            st["mid"] = mix(x, jnp.concatenate(st["att"], axis=0), 1)
+            x, y = far_half(ws), list(st["att"])
+            if nwin - 1 in ws:
+                x, y = x + own_half([nwin - 1]), y + [att[nwin - 1]]
+            st["mid"] = mix(jnp.concatenate(x, axis=0).astype(f32), jnp.concatenate(y, axis=0), 1)
 
         def close():
-            for w, y in zip(ws, split_rows(feed(*st["mid"], 1))):
-                yr[w] = y
-            for i in ids:
-                back(i).start()
-            if nwin - 1 in ws:
-                fringe[1].start()
+            mid, normed = st["mid"]
+            start = 0
+            for p, ids in parts:
+                tail = nwin - 1 in p
+                end = start + (len(p) + tail) * 2 * PART
+                ys = split_rows(feed(mid[start:end], normed[start:end], 1))
+                for w, y in zip(p, ys):
+                    yr[w] = y
+                if tail:
+                    yo[nwin] = ys[-1]
+                start = end
+                for i in ids:
+                    back(i).start()
+                if tail:
+                    for c in fringe:
+                        c.start()
 
         return {"wait": wait, "score": score, "soften": soften, "middle": middle, "close": close}
 
     def own(ws):
-        st = {}
-
-        def wait():
-            pass
-
-        def score():
-            st["triple"] = jnp.concatenate([tri[w] for w in ws], axis=0)
-            st["scores"] = scores_of(st["triple"], hmask, heads, near)
-
-        def soften():
-            st["att"] = blend(weigh(st["scores"], bias[1, near, :], masks(ws, near)), st["triple"], hmask, heads)
-
-        def middle():
-            x = jnp.concatenate(own_half(ws), axis=0).astype(f32)
-            st["mid"] = mix(x, jnp.concatenate(st["att"], axis=0), 1)
-
-        def close():
-            for w, y in zip(ws, split_rows(feed(*st["mid"], 1))):
-                yo[w + 1] = y
-            if nwin - 1 in ws:
-                fringe[0].start()
-
-        return {"wait": wait, "score": score, "soften": soften, "middle": middle, "close": close}
-
-    last = chunks - 1
-    first = [block0(k) for k in range(last, -1, -1)]
+        x = jnp.concatenate(own_half(ws), axis=0).astype(f32)
+        for w, y in zip(ws, split_rows(feed(*mix(x, gather(att, ws), 1), 1))):
+            yo[w + 1] = y
+
+    first = [block0([[0, 1], [2]])] + [block0([[i]]) for i in range(3, len(heads_of))]
     bring(0, (0,))
+    settle(0, (0,))
     overlap(first[0], None)
     bring(0, (1, 2, 3))
+    first[0]["middle"]()
+    first[1]["score"]()
+    settle(0, (1, 2, 3))
+    first[0]["close"]()
+    bring(1, range(4))
+    first[1]["soften"]()
+    for t in range(1, chunks):
+        overlap(first[t + 1] if t < chunks - 1 else None, first[t])
     regions()
-    first[0]["middle"]()
-    settle(0)
-    first[0]["close"]()
-    first[1]["score"]()
-    first[1]["soften"]()
-    bring(1, range(4))
+    settle(1, range(4))
+    second = [block1([[0]], [halo(1), halo(2)] + edges)]
+    second += [block1([[i]], [halo(i + 2)]) for i in range(1, chunks - 1)]
+    second += [block1([[chunks - 1], [chunks]], [halo(0), halo(chunks + 1)])]
+    overlap(second[0], None)
+    pl.semaphore_wait(ready, 2)
     for t in range(1, chunks):
-        overlap(first[t + 1] if t < last else None, first[t])
-    settle(1)
-    second = [block1([k], [halo(k)]) for k in range(last, 0, -1)] + [block1([0, chunks], [halo(0)] + edges)]
+        overlap(second[t], second[t - 1])
+    overlap(None, second[-1])
     half = nwin // 2
-    second += [own([nwin - 1] + list(range(half - 1))), own(list(range(half - 1, nwin - 1)))]
-    for t in range(len(second) + 1):
-        overlap(second[t] if t < len(second) else None, second[t - 1] if t > 0 else None)
+    own(list(range(half)))
+    own(list(range(half, nwin - 1)))
 
     def place(src, base):
         v = src[...].astype(f32)
@@ -464,17 +491,17 @@
                 o_ref[base + 2 * i + r] = y.reshape(cols, width).astype(bf16)
 
     fringe[0].wait_recv()
-    place(yo, SHIFT)
-    for k in range(chunks + 1):
-        back(k).wait_recv()
-    fringe[1].wait_recv()
-    place(yt, 0)
+    place(yo, 0)
     for c in labels + smalls + edges + fringe + list(direct.values()) + list(relays.values()):
         c.wait_send()
-    for k in range(chunks):
-        halo(k).wait_send()
-    for k in range(chunks + 1):
-        back(k).wait_send()
+    for i in range(len(heads_of)):
+        halo(i).wait_send()
+    for i in range(len(spans)):
+        back(i).wait_send()
+    for i in range(len(spans)):
+        back(i).wait_recv()
+    fringe[1].wait_recv()
+    place(yt, SHIFT)
 
 
 def on_device(*args):
@@ -501,14 +528,15 @@
         vm((n,) + args[7].shape, f32), vm((n,) + args[6].shape, f32), vm((n,) + args[11].shape, f32),
         vm((BLOCKS, 1, 3 * width), f32), vm((BLOCKS, 1, hidden), f32), vm((BLOCKS, KEYS, heads * KEYS), f32),
         vm((3, rows, cols), i32), vm((KEYS, 128), f32), vm((128, 128), f32),
-        vm((nwin, KEYS, width), bf16), vm((nwin, KEYS, width), bf16), vm((nwin, KEYS, 3 * width), bf16),
+        vm((nwin, KEYS, width), bf16), vm((nwin, KEYS, width), bf16), vm((nwin, 2 * PART, width), bf16),
         vm((nwin + 1, KEYS, width), bf16), vm((nwin + 1, 2 * PART, width), bf16),
         vm((nwin, 2 * PART, width), bf16), vm((nwin + 1, 2 * PART, width), bf16),
         vm((nwin + 1, 2 * PART, width), bf16),
         dma((14,)), dma((n - 1, 3)), dma((n - 1, 3)), dma((n - 1, BLOCKS, 4)), dma((n - 1, BLOCKS, 4)),
         dma((n - 1, BLOCKS, 4)), dma((n - 1, BLOCKS, 4)), dma((3,)), dma((3,)),
-        dma((chunks,)), dma((chunks,)), dma((2,)), dma((2,)),
+        dma((chunks + 2,)), dma((chunks + 2,)), dma((2,)), dma((2,)),
         dma((chunks + 1,)), dma((chunks + 1,)), dma((2,)), dma((2,)),
+        pltpu.SemaphoreType.REGULAR,
     ]
     return pl.pallas_call(
         functools.partial(fused, heads, group),

time: 30.1 us -> 28.4 us (0.944)
  Pallas kernels: 29.1 us -> 27.5 us
    pallas_call x1, Pallas kernels: 29.1 us -> 27.5 us  [on_device(): pl.pallas_call(functools.partial(fused, heads, group), out_shape=vm(x.sha...]
where the time goes in v3:
time: 28.4 us; the launch traced here: 28.3 us
  Pallas kernels  27.5 us (97%)
  local copies, waits for them, and re-layouts  0.8 us (3%)
    pallas_call x1, Pallas kernels, on_device(): pl.pallas_call(functools.partial(fused, heads, group), out_shape=vm(x.sha...  27.5 us
    unnamed x1, local copies, waits for them, and re-layouts  0.8 us

profile of v3, /device:TPU:0, one launch (start us, length us, event | category | flops | bytes accessed | tf_op | source)
XLA Modules:
  0.0 28.3 jit_solution(6368021678780736065)
XLA Ops:
  0.0 27.5 %fused.1 = bf16[8,256,128]{2,1,0:T(8,128)(2,1)S(1)} custom-call(bf16[8,256,128]{2,1,0:T(8,128)(2,1)} %x_h.1, s32[8,256]{1,0:T(8,128)} %lab_h.1, s32[64,64]{1,0:T(8,128)} %rel_h.1, f32[2,2,128]{2,1,0:T(2,128)} %gain_h.1, f32[2,2,128]{2,1,0:T(2,128)} %shift_h.1, bf16[2,3,64,128]{3,2,1,0:T(8,128)(2,1)} %bitcast.3, f32[3,2,64]{2,1,0:T(2,128)} %bitcast.5, ...), custom_call_target="tpu_custom_call" | custom-call | tf_op jit(solution)/shard_map/fused/pallas_call | solution.py:541
  27.5 0.8 %copy.16 = bf16[8,256,128]{2,1,0:T(8,128)(2,1)} copy(bf16[8,256,128]{2,1,0:T(8,128)(2,1)S(1)} %fused.1) | data formatting | bytes 1048576

commit v4 on v3

--- a/solution.py
+++ b/solution.py
@@ -123,8 +123,7 @@
     x_v, lab, rel, gain, shift, proj_b, fc2_b,
     qkv, proj, fc1, fc2, tab_all, qb_all, f1b_all, qb, f1b, bias, lab3, rt, ru,
     xq, nq, att, x1, above, yr, yt, yo,
-    in_sem, ssend, srecv, wsend, wrecv, rsend, rrecv, lsend, lrecv, hsend, hrecv, esend, erecv,
-    osend, orecv, fsend, frecv, ready,
+    in_sem, extra, srecv, wsend, wrecv, rsend, rrecv, lsend, lrecv, hrecv, erecv, orecv, frecv, ready,
 ):
     rows, cols, width = x_v.shape
     nwin = cols // WIN
@@ -195,14 +194,16 @@
         for b in range(BLOCKS):
             share, count, others = shares[b]
             for i, s in enumerate(slots(b, ch, share, count)):
-                direct[d, b, i] = remote(s, s, wsend.at[d - 1, b, i], wrecv.at[d - 1, b, i], to)
+                sent = wsend.at[d - 1, i] if b else in_sem.at[3 + i] if d == 1 else extra.at[7 * (d - 2) + 3 + i]
+                direct[d, b, i] = remote(s, s, sent, wrecv.at[d - 1, b, i], to)
             for e, other in enumerate(others):
                 for i, s in enumerate(slots(b, owner, share, count)):
                     if (b, i) not in WHOLE:
                         r = b + e
                         relays[d, b, i, e] = remote(s, s, rsend.at[d - 1, r, i], rrecv.at[d - 1, r, i], other)
         for i, ref in enumerate([tab_all, qb_all, f1b_all]):
-            smalls.append(remote(ref.at[ch], ref.at[ch], ssend.at[d - 1, i], srecv.at[d - 1, i], to))
+            sent = in_sem.at[i] if d == 1 else extra.at[7 * (d - 2) + i]
+            smalls.append(remote(ref.at[ch], ref.at[ch], sent, srecv.at[d - 1, i], to))
     loads["lab"].wait()
     labels = []
     for i, d in enumerate(around[:3]):
@@ -260,11 +261,10 @@
             bias[b, :, t * 128 : (t + 1) * 128] = jnp.where(lane < KEYS, out[0], out[1]) * LOG2E
 
     hmask = head_mask(heads, KEYS, width)
-    lanes3 = lax.broadcasted_iota(i32, (1, 3 * width), 1)
-    mult = jnp.where(lanes3 < width, scale, 1.0)
 
     def project(normed, b):
-        return ((dot_t(normed, rows_of(qkv[b])) + qb[b]) * mult).astype(bf16)
+        out = dot_t(normed, rows_of(qkv[b])) + qb[b]
+        return jnp.concatenate([(out[:, :width] * scale).astype(bf16), out[:, width:].astype(bf16)], axis=1)
 
     def regions():
         for c in labels:
@@ -301,11 +301,16 @@
         middle = (x + dot(attended, proj[b]) + proj_b[b : b + 1]).astype(bf16).astype(f32)
         return middle, layer_norm(middle, gain[b, 1:2], shift[b, 1:2])
 
-    def feed(middle, normed, b):
+    def widen(normed, b):
         inner = (dot(normed, fc1[b]) + f1b[b]).astype(bf16)
-        hidden = inner * (lax.erf(inner * bf16(0.5 ** 0.5)) + bf16(1.0))
+        return inner * (lax.erf(inner * bf16(0.5 ** 0.5)) + bf16(1.0))
+
+    def narrow(middle, hidden, b):
         outer = dot(hidden, fc2[b] * bf16(0.5))
         return (middle + outer + fc2_b[b : b + 1]).astype(bf16)
+
+    def feed(middle, normed, b):
+        return narrow(middle, widen(normed, b), b)
 
     cut = group // 2
     final = nwin - group
@@ -315,11 +320,11 @@
     def halo(i):
         start, size = heads_of[i]
         span = pl.ds(start, size)
-        return remote(x1.at[span, 2 * PART :, :], above.at[span], hsend.at[i], hrecv.at[i], at(1, 0))
+        return remote(x1.at[span, 2 * PART :, :], above.at[span], in_sem.at[8 + i], hrecv.at[i], at(1, 0))
 
     edges = [
-        remote(x1.at[0, :PART], x1.at[nwin, :PART], esend.at[0], erecv.at[0], at(0, -1)),
-        remote(x1.at[0, 2 * PART : 3 * PART], above.at[nwin, :PART], esend.at[1], erecv.at[1], at(1, -1)),
+        remote(x1.at[0, :PART], x1.at[nwin, :PART], lsend.at[0], erecv.at[0], at(0, -1)),
+        remote(x1.at[0, 2 * PART : 3 * PART], above.at[nwin, :PART], lsend.at[1], erecv.at[1], at(1, -1)),
     ]
 
     spans = [(k * group, group) for k in range(chunks - 1, 0, -1)] + [(0, cut), (cut, group - cut)]
@@ -327,12 +332,12 @@
     def back(i):
         start, size = spans[i]
         return remote(
-            yr.at[pl.ds(start, size)], yt.at[pl.ds(start + 1, size)], osend.at[i], orecv.at[i], at(-1, 0)
+            yr.at[pl.ds(start, size)], yt.at[pl.ds(start + 1, size)], in_sem.at[i], orecv.at[i], at(-1, 0)
         )
 
     fringe = [
-        remote(yo.at[nwin, PART :], yo.at[0, PART :], fsend.at[0], frecv.at[0], at(0, 1)),
-        remote(yr.at[nwin - 1, PART :], yt.at[0, PART :], fsend.at[1], frecv.at[1], at(-1, 1)),
+        remote(yo.at[nwin, PART :], yo.at[0, PART :], in_sem.at[chunks + 1], frecv.at[0], at(0, 1)),
+        remote(yr.at[nwin - 1, PART :], yt.at[0, PART :], in_sem.at[chunks + 2], frecv.at[1], at(-1, 1)),
     ]
 
     def bring(b, pieces):
@@ -372,12 +377,17 @@
         def middle():
             st["mid"] = mix(gather(xq, ws).astype(f32), jnp.concatenate(st["att"], axis=0), 0)
 
+        def expand():
+            st["hidden"] = widen(st["mid"][1], 0)
+
         def close():
-            mid, normed = st["mid"]
+            mid = st["mid"][0]
+            if "hidden" not in st:
+                expand()
             start = 0
             for p, ids in parts:
                 end = start + len(p) * KEYS
-                y = feed(mid[start:end], normed[start:end], 0)
+                y = narrow(mid[start:end], st["hidden"][start:end], 0)
                 for g, w in enumerate(p):
                     x1[w] = y[g * KEYS : (g + 1) * KEYS]
                 start = end
@@ -387,7 +397,9 @@
                     for c in edges:
                         c.start()
 
-        return {"wait": wait, "score": score, "soften": soften, "middle": middle, "close": close}
+        return {
+            "wait": wait, "score": score, "soften": soften, "middle": middle, "expand": expand, "close": close,
+        }
 
     def own_half(ws):
         return sum([[x1[w, PART : 2 * PART], x1[w + 1, :PART]] for w in ws], [])
@@ -459,11 +471,17 @@
     first = [block0([[0, 1], [2]])] + [block0([[i]]) for i in range(3, len(heads_of))]
     bring(0, (0,))
     settle(0, (0,))
-    overlap(first[0], None)
-    bring(0, (1, 2, 3))
+    first[0]["score"]()
+    bring(0, (1, 2))
+    first[0]["soften"]()
+    bring(0, (3,))
     first[0]["middle"]()
+    settle(0, (2,))
+    first[0]["expand"]()
     first[1]["score"]()
-    settle(0, (1, 2, 3))
+    for c in labels:
+        c.wait_send()
+    settle(0, (3,))
     first[0]["close"]()
     bring(1, range(4))
     first[1]["soften"]()
@@ -476,12 +494,14 @@
     second += [block1([[chunks - 1], [chunks]], [halo(0), halo(chunks + 1)])]
     overlap(second[0], None)
     pl.semaphore_wait(ready, 2)
+    for c in smalls + [c for (_, b, _), c in direct.items() if b == 0]:
+        c.wait_send()
+    own(list(range(final, nwin - 1)))
     for t in range(1, chunks):
         overlap(second[t], second[t - 1])
     overlap(None, second[-1])
     half = nwin // 2
-    own(list(range(half)))
-    own(list(range(half, nwin - 1)))
+    own(list(range(final)))
 
     def place(src, base):
         v = src[...].astype(f32)
@@ -492,7 +512,7 @@
 
     fringe[0].wait_recv()
     place(yo, 0)
-    for c in labels + smalls + edges + fringe + list(direct.values()) + list(relays.values()):
+    for c in edges + fringe + [c for (_, b, _), c in direct.items() if b] + list(relays.values()):
         c.wait_send()
     for i in range(len(heads_of)):
         halo(i).wait_send()
@@ -532,10 +552,9 @@
         vm((nwin + 1, KEYS, width), bf16), vm((nwin + 1, 2 * PART, width), bf16),
         vm((nwin, 2 * PART, width), bf16), vm((nwin + 1, 2 * PART, width), bf16),
         vm((nwin + 1, 2 * PART, width), bf16),
-        dma((14,)), dma((n - 1, 3)), dma((n - 1, 3)), dma((n - 1, BLOCKS, 4)), dma((n - 1, BLOCKS, 4)),
+        dma((10 + max(4, chunks),)), dma((max(1, 7 * (n - 2)),)), dma((n - 1, 3)), dma((n - 1, 4)), dma((n - 1, BLOCKS, 4)),
         dma((n - 1, BLOCKS, 4)), dma((n - 1, BLOCKS, 4)), dma((3,)), dma((3,)),
-        dma((chunks + 2,)), dma((chunks + 2,)), dma((2,)), dma((2,)),
-        dma((chunks + 1,)), dma((chunks + 1,)), dma((2,)), dma((2,)),
+        dma((chunks + 2,)), dma((2,)), dma((chunks + 1,)), dma((2,)),
         pltpu.SemaphoreType.REGULAR,
     ]
     return pl.pallas_call(

time: 28.4 us -> 28.4 us (level)
  no operation moved by 1% of the time
where the time goes in v4:
time: 28.4 us; the launch traced here: 28.2 us
  Pallas kernels  27.4 us (96%)
  local copies, waits for them, and re-layouts  0.8 us (3%)
    pallas_call x1, Pallas kernels, on_device(): pl.pallas_call(functools.partial(fused, heads, group), out_shape=vm(x.sha...  27.4 us
    unnamed x1, local copies, waits for them, and re-layouts  0.8 us

profile of v4, /device:TPU:0, one launch (start us, length us, event | category | flops | bytes accessed | tf_op | source)
XLA Modules:
  0.0 28.2 jit_solution(14694568228719058444)
XLA Ops:
  0.0 27.4 %fused.1 = bf16[8,256,128]{2,1,0:T(8,128)(2,1)S(1)} custom-call(bf16[8,256,128]{2,1,0:T(8,128)(2,1)} %x_h.1, s32[8,256]{1,0:T(8,128)} %lab_h.1, s32[64,64]{1,0:T(8,128)} %rel_h.1, f32[2,2,128]{2,1,0:T(2,128)} %gain_h.1, f32[2,2,128]{2,1,0:T(2,128)} %shift_h.1, bf16[2,3,64,128]{3,2,1,0:T(8,128)(2,1)} %bitcast.3, f32[3,2,64]{2,1,0:T(2,128)} %bitcast.5, ...), custom_call_target="tpu_custom_call" | custom-call | tf_op jit(solution)/shard_map/fused/pallas_call | solution.py:560
  27.4 0.8 %copy.16 = bf16[8,256,128]{2,1,0:T(8,128)(2,1)} copy(bf16[8,256,128]{2,1,0:T(8,128)(2,1)S(1)} %fused.1) | data formatting | bytes 1048576

commit v5 on v4

--- a/solution.py
+++ b/solution.py
@@ -298,11 +298,11 @@
         rt[...] = kinds[:KEYS]
 
     def mix(x, attended, b):
-        middle = (x + dot(attended, proj[b]) + proj_b[b : b + 1]).astype(bf16).astype(f32)
+        middle = (x + dot(attended, proj[b]) + proj_b[b : b + 1])
         return middle, layer_norm(middle, gain[b, 1:2], shift[b, 1:2])
 
     def widen(normed, b):
-        inner = (dot(normed, fc1[b]) + f1b[b]).astype(bf16)
+        inner = dot(normed, fc1[b]).astype(bf16) + f1b[b].astype(bf16)
         return inner * (lax.erf(inner * bf16(0.5 ** 0.5)) + bf16(1.0))
 
     def narrow(middle, hidden, b):

time: 28.4 us -> 28.4 us (level)
  no operation moved by 1% of the time
where the time goes in v5:
time: 28.4 us; the launch traced here: 28.2 us
  Pallas kernels  27.4 us (96%)
  local copies, waits for them, and re-layouts  0.8 us (3%)
    pallas_call x1, Pallas kernels, on_device(): pl.pallas_call(functools.partial(fused, heads, group), out_shape=vm(x.sha...  27.4 us
    unnamed x1, local copies, waits for them, and re-layouts  0.8 us

profile of v5, /device:TPU:0, one launch (start us, length us, event | category | flops | bytes accessed | tf_op | source)
XLA Modules:
  0.0 28.2 jit_solution(4865830217123313207)
XLA Ops:
  0.0 27.4 %fused.1 = bf16[8,256,128]{2,1,0:T(8,128)(2,1)S(1)} custom-call(bf16[8,256,128]{2,1,0:T(8,128)(2,1)} %x_h.1, s32[8,256]{1,0:T(8,128)} %lab_h.1, s32[64,64]{1,0:T(8,128)} %rel_h.1, f32[2,2,128]{2,1,0:T(2,128)} %gain_h.1, f32[2,2,128]{2,1,0:T(2,128)} %shift_h.1, bf16[2,3,64,128]{3,2,1,0:T(8,128)(2,1)} %bitcast.3, f32[3,2,64]{2,1,0:T(2,128)} %bitcast.5, ...), custom_call_target="tpu_custom_call" | custom-call | tf_op jit(solution)/shard_map/fused/pallas_call | solution.py:560
  27.4 0.8 %copy.16 = bf16[8,256,128]{2,1,0:T(8,128)(2,1)} copy(bf16[8,256,128]{2,1,0:T(8,128)(2,1)S(1)} %fused.1) | data formatting | bytes 1048576
